TPU v7x, 256 devices: a whole 4x4x8 slice. The times are simulated.
256 devices in a mesh: node: 2 (over y_lo), space: 128 (over y_hi, x, z, core).
Axes of the slice: x: 4, y: 4 (y_hi: 2, y_lo: 2; y = y_hi * 2 + y_lo), z: 8, core: 2. Of those that a mesh axis runs over, the one named last changes fastest.
Arguments:
- u_start: float32 [1024, 256, 128], P('space'), may hold values from 0 to 1
- v_start: float32 [1024, 256, 128], P('space'), may hold values from 0 to 2
- labels: int32 [1024, 256, 128], P('space'), may hold values from 0 to 2
- u_guess: float32 [4, 1024, 256, 128], P('node', 'space'), may hold values from 0 to 1
- v_guess: float32 [4, 1024, 256, 128], P('node', 'space'), may hold values from 0 to 2
Outputs:
- u_nodes: float32 [4, 1024, 256, 128], P('node', 'space')
- v_nodes: float32 [4, 1024, 256, 128], P('node', 'space')
Inputs may be any that keep to these rules, and one draw needn't show every extreme that they name: `labels`: 0 marks healthy, 1 fibrous and 2 scar tissue.
All inputs are finite; a program needn't handle non-finite values.
Results may differ from a plain program's by a relative error of at most 0.0001.
Values sent between devices are 32-bit elements; how exact they have to be, the bound alone decides.
A program may use at most 192 MiB of HBM per device.

v0:
```python
import jax
import jax.numpy as jnp
from jax import lax
from jax.sharding import PartitionSpec as P

SWEEPS = 2


radau_points = (0.08858795951270396, 0.4094668644407347, 0.7876594617608471, 1.0)
time_step = 0.16
onset_level = 0.15
ionic_gain = 8.0
recovery_base = 0.002
recovery_slope = 0.2
recovery_offset = 0.3
conductances = (1.0, 0.35, 0.05)
excitability = (1.0, 0.6, 0.0)


def with_halo(block, sides, width):
    for axis, dim in sides:
        count = lax.axis_size(axis)
        forward = [(i, i + 1) for i in range(count - 1)]
        backward = [(target, source) for source, target in forward]
        low = lax.ppermute(
            lax.slice_in_dim(block, block.shape[dim] - width, None, axis=dim), axis, forward
        )
        high = lax.ppermute(lax.slice_in_dim(block, 0, width, axis=dim), axis, backward)
        block = jnp.concatenate([low, block, high], axis=dim)
    return block


def laid_out(parts, dim):
    dims = list(parts.shape[1:])
    dims[dim] *= parts.shape[0]
    return jnp.moveaxis(parts, 0, dim).reshape(dims)


def from_everyone(shard, axis):
    count = lax.axis_size(axis)
    return lax.all_to_all(
        jnp.broadcast_to(shard[None], (count, *shard.shape)), axis, 0, 0, tiled=True
    )


def gather_directly(shard, axis, dim):
    return laid_out(from_everyone(shard, axis), dim)


def sent_together(arrays, axis, dim, along):
    ends, at = ([], 0)
    for a in arrays[:-1]:
        at += a.shape[along]
        ends.append(at)
    both = jnp.concatenate(arrays, axis=along)
    return tuple(jnp.split(gather_directly(both, axis, dim), ends, axis=along))


def weight_table():
    table = []
    for target in range(4):
        entries = []
        for column in range(4):
            coeffs = [1.0]
            for other in range(4):
                if other != column:
                    factor = 1.0 / (radau_points[column] - radau_points[other])
                    raised = [0.0] + coeffs
                    lowered = coeffs + [0.0]
                    coeffs = [
                        factor * (raised[place] - radau_points[other] * lowered[place])
                        for place in range(len(raised))
                    ]
            integral = 0.0
            for place in range(len(coeffs)):
                integral = integral + coeffs[place] * radau_points[target] ** (place + 1) / (
                    place + 1
                )
            entries.append(time_step * integral)
        table.append(entries)
    return table


def label_values(labels, values):
    return jnp.where(
        labels == 0,
        jnp.float32(values[0]),
        jnp.where(labels == 1, jnp.float32(values[1]), jnp.float32(values[2])),
    )


def face_terms(conduct_ext):
    padded = jnp.pad(conduct_ext, ((0, 0), (1, 1), (1, 1)))
    center = padded[1:-1, 1:-1, 1:-1]
    sides = (
        padded[2:, 1:-1, 1:-1],
        padded[:-2, 1:-1, 1:-1],
        padded[1:-1, 2:, 1:-1],
        padded[1:-1, :-2, 1:-1],
        padded[1:-1, 1:-1, 2:],
        padded[1:-1, 1:-1, :-2],
    )
    result = []
    for beside in sides:
        total = center + beside
        result.append(
            jnp.where(total > 0, 2.0 * center * beside / jnp.where(total > 0, total, 1.0), 0.0)
        )
    return result


def rates(u_ext, v_field, facing, excite):
    padded = jnp.pad(u_ext, ((0, 0), (0, 0), (1, 1), (1, 1)))
    u_field = padded[:, 1:-1, 1:-1, 1:-1]
    sides = (
        padded[:, 2:, 1:-1, 1:-1],
        padded[:, :-2, 1:-1, 1:-1],
        padded[:, 1:-1, 2:, 1:-1],
        padded[:, 1:-1, :-2, 1:-1],
        padded[:, 1:-1, 1:-1, 2:],
        padded[:, 1:-1, 1:-1, :-2],
    )
    spread = jnp.zeros_like(u_field)
    for face_value, voltage_side in zip(facing, sides):
        spread = spread + face_value[None] * (voltage_side - u_field)
    ionic = ionic_gain * u_field * (u_field - onset_level) * (1.0 - u_field) - u_field * v_field
    rate_u = spread + excite[None] * ionic
    recovery = recovery_base + recovery_slope * v_field / jnp.maximum(
        u_field + recovery_offset, recovery_offset
    )
    rate_v = recovery * (-v_field - ionic_gain * u_field * (u_field - onset_level - 1.0))
    return (rate_u, rate_v)


def on_device(u_start, v_start, labels, u_guess, v_guess):
    local_nodes = u_guess.shape[0]
    first_node = lax.axis_index("node") * local_nodes
    weights_all = jnp.asarray(weight_table(), jnp.float32)
    conduct = label_values(labels, conductances)
    excite = label_values(labels, excitability)
    reach = 1
    tissue = with_halo(jnp.stack([conduct, excite]), (("space", 1),), reach)
    u_nodes, v_nodes = sent_together((u_guess, v_guess), "node", 0, 1)
    facing = face_terms(tissue[0])
    excite_mid = tissue[1, 1:-1]
    u_now, v_now = (u_nodes, v_nodes)
    for sweep_index in range(SWEEPS):
        bordered = with_halo(u_now, (("space", 1),), 1)
        rate_u, rate_v = rates(bordered, v_now, facing, excite_mid)
        summed_u = jnp.einsum("ij,jabc->iabc", weights_all, rate_u, precision=lax.Precision.HIGHEST)
        summed_v = jnp.einsum("ij,jabc->iabc", weights_all, rate_v, precision=lax.Precision.HIGHEST)
        u_now = u_start[None] + summed_u
        v_now = v_start[None] + summed_v
    u_now = lax.dynamic_slice_in_dim(u_now, first_node, local_nodes, 0)
    v_now = lax.dynamic_slice_in_dim(v_now, first_node, local_nodes, 0)
    return (u_now, v_now)


def solution(mesh):
    return jax.shard_map(
        on_device,
        mesh=mesh,
        in_specs=(
            P("space", None, None),
            P("space", None, None),
            P("space", None, None),
            P("node", "space", None, None),
            P("node", "space", None, None),
        ),
        out_specs=(P("node", "space", None, None), P("node", "space", None, None)),
        check_vma=False,
    )
```

profile of v0, /device:TPU:231, one launch (start us, length us, event | category | flops | bytes accessed | tf_op | source)
XLA Modules:
  0.0 236.9 jit_solution(15570286790418096519)
XLA Ops:
  0.6 2.5 %pad_maximum_fusion.4 = f32[2,16,256,128]{3,2,1,0:T(8,128)S(1)} fusion(f32[2,8,256,128]{3,2,1,0:T(8,128)} %param.10, f32[2,8,256,128]{3,2,1,0:T(8,128)} %param.9), kind=kLoop, calls=%fused_computation.55 | loop fusion | flops 1048576 | bytes 8388608 | tf_op jit(solution)/shard_map/concatenate | solution.py:55
  3.1 3.2 %copy.11 = f32[2,16,256,128]{3,0,2,1:T(2,128)S(1)} copy(f32[2,16,256,128]{3,2,1,0:T(8,128)S(1)} %pad_maximum_fusion.4) | data formatting | bytes 8388608 | tf_op jit(solution)/shard_map/concatenate | solution.py:55
  6.4 4.2 %broadcast_in_dim.65 = f32[2,2,16,256,128]{4,1,3,2,0:T(2,128)} broadcast(f32[2,16,256,128]{3,0,2,1:T(2,128)S(1)} %copy.11), dimensions={1,2,3,4} | broadcast | bytes 12582912 | tf_op jit(solution)/shard_map/broadcast_in_dim | solution.py:42
  10.6 7.1 %all-to-all-start = ((f32[2,2,16,256,128]{4,1,3,2,0:T(2,128)}), f32[2,2,16,256,128]{4,1,3,2,0:T(2,128)}, u32[]{:S(2)}, u32[]{:S(2)}) async-start(f32[2,2,16,256,128]{4,1,3,2,0:T(2,128)} %broadcast_in_dim.65), calls=%async_computation | async-start | bytes 16777216 | tf_op jit(solution)/shard_map/all_to_all | solution.py:41
  17.7 0.4 fusion.110
  18.1 0.2 fusion.111
  18.3 0.7 pad_maximum_fusion.12
  19.0 2.6 %collective-permute-start = (f32[2,1,256,128]{3,2,1,0:T(8,128)}, f32[2,1,256,128]{3,2,1,0:T(8,128)S(1)}, u32[]{:S(2)}, u32[]{:S(2)}) collective-permute-start(f32[2,1,256,128]{3,2,1,0:T(8,128)} %get-tuple-element.16), channel_id=1, source_target_pairs={{1,0},{2,1},{3,2},{4,3},{5,4},{6,5},{7,6},{8,7},{9,8},{10,9},{11,1... | collective-permute-start | bytes 786440 | tf_op jit(solution)/shard_map/ppermute | solution.py:28
  21.6 8.7 %collective-permute-start.2 = (f32[2,1,256,128]{3,2,1,0:T(8,128)S(1)}, f32[2,1,256,128]{3,2,1,0:T(8,128)S(1)}, u32[]{:S(2)}, u32[]{:S(2)}) collective-permute-start(f32[2,1,256,128]{3,2,1,0:T(8,128)S(1)} %get-tuple-element.15), channel_id=1, source_target_pairs={{0,1},{1,2},{2,3},{3,4},{4,5},{5,6},{6,7},{7,8},{8,9},{9,10},{10,1... | collective-permute-start | bytes 786440 | tf_op jit(solution)/shard_map/ppermute | solution.py:25
  30.3 2.4 %collective-permute-done = f32[2,1,256,128]{3,2,1,0:T(8,128)S(1)} collective-permute-done((f32[2,1,256,128]{3,2,1,0:T(8,128)}, f32[2,1,256,128]{3,2,1,0:T(8,128)S(1)}, u32[]{:S(2)}, u32[]{:S(2)}) %collective-permute-start) | collective-permute-done | bytes 262176 | tf_op jit(solution)/shard_map/ppermute | solution.py:28
  32.7 0.9 collective-permute-done.2
  33.7 1.9 fusion.102
  35.6 3.8 %compare_select_fusion.6 = (f32[8,256,128]{2,1,0:T(8,128)}, f32[8,256,128]{2,1,0:T(8,128)}, f32[8,256,128]{2,1,0:T(8,128)}, f32[8,256,128]{2,1,0:T(8,128)}, f32[8,256,128]{2,1,0:T(8,128)}) fusion(f32[10,256,128]{2,1,0:T(8,128)S(1)} %fusion.100, pred[8,256,128]{2,1,0:T(8,128)(4,1)S(1)} %get-tuple-element.8, pred[8,256,128]{2,1,0:T(8,128)(4,1)S(1)} %get-tuple-element.7), kind=kLoop, calls=%fused_computation.132 | loop fusion | flops 7602176 | bytes 7077888 | tf_op jit(solution)/shard_map/jit(_where)/select_n | solution.py:107
  39.4 70.0 %all-to-all-done = f32[2,2,16,256,128]{4,1,3,2,0:T(2,128)} async-done(((f32[2,2,16,256,128]{4,1,3,2,0:T(2,128)}), f32[2,2,16,256,128]{4,1,3,2,0:T(2,128)}, u32[]{:S(2)}, u32[]{:S(2)}) %all-to-all-start) | async-done | bytes 8388640 | tf_op jit(solution)/shard_map/all_to_all | solution.py:41
  109.4 5.4 %copy.12 = f32[2,2,16,256,128]{4,1,0,3,2:T(2,128)S(1)} copy(f32[2,2,16,256,128]{4,1,3,2,0:T(2,128)} %all-to-all-done) | data formatting | bytes 16777216 | tf_op jit(solution)/shard_map/all_to_all | solution.py:41
  114.9 3.4 %collective-permute-start.1 = (f32[4,1,256,128]{3,0,2,1:T(4,128)S(1)}, f32[4,1,256,128]{3,0,2,1:T(4,128)S(1)}, u32[]{:S(2)}, u32[]{:S(2)}) collective-permute-start(f32[4,1,256,128]{3,0,2,1:T(4,128)S(1)} %get-tuple-element.10), channel_id=1, source_target_pairs={{1,0},{2,1},{3,2},{4,3},{5,4},{6,5},{7,6},{8,7},{9,8},{10,9},{11,1... | collective-permute-start | bytes 1572872 | tf_op jit(solution)/shard_map/ppermute | solution.py:28
  118.3 8.0 %collective-permute-start.3 = (f32[4,1,256,128]{3,0,2,1:T(4,128)S(1)}, f32[4,1,256,128]{3,0,2,1:T(4,128)S(1)}, u32[]{:S(2)}, u32[]{:S(2)}) collective-permute-start(f32[4,1,256,128]{3,0,2,1:T(4,128)S(1)} %get-tuple-element.9), channel_id=1, source_target_pairs={{0,1},{1,2},{2,3},{3,4},{4,5},{5,6},{6,7},{7,8},{8,9},{9,10},{10,1... | collective-permute-start | bytes 1572872 | tf_op jit(solution)/shard_map/ppermute | solution.py:25
  126.4 11.9 %fusion.43 = f32[8,256,128,4]{2,3,1,0:T(4,128)} fusion(f32[4,4,1,1]{1,0,3,2:T(4,128)S(1)} %copy-done.8, f32[4,16,256,128]{3,0,2,1:T(4,128)S(1)} %bitcast.53), kind=kOutput, calls=%fused_computation.69 | convolution fusion | flops 61865984 | bytes 12582976 | tf_op jit(solution)/shard_map/ij,jabc->iabc/dot_general | solution.py:151
  138.3 0.3 split.8
  138.6 10.6 %select_maximum_fusion.2 = f32[4,10,258,130]{3,0,2,1:T(4,128)} fusion(f32[4,1,256,128]{3,0,2,1:T(4,128)S(1)} %collective-permute-done.1, f32[4,8,256,128]{3,0,2,1:T(4,128)S(1)} %split.8, f32[4,1,256,128]{3,0,2,1:T(4,128)S(1)} %collective-permute-done.3), kind=kLoop, calls=%fused_computation.6 | loop fusion | flops 20124000 | bytes 10609280 | tf_op jit(solution)/shard_map/concatenate | solution.py:29
  149.2 22.0 %add_bitcast_fusion = f32[4,8,256,128]{3,0,2,1:T(4,128)} fusion(f32[4,4,1,1]{1,0,3,2:T(4,128)S(1)} %copy-done.8, f32[4,8,256,128]{3,0,2,1:T(4,128)S(1)} %split.8, f32[4,10,258,130]{3,0,2,1:T(4,128)} %select_maximum_fusion.2, f32[4,1,256,128]{3,0,2,1:T(4,128)} %copy-done.7, f32[4,1,256,128]{3,0,2,1:T(4,128)S(1)} %collective-permute-done.1, ...), kind=kOutput, calls=%fused_computation.79 | convolution fusion | flops 80740352 | bytes 38799360 | tf_op jit(solution)/shard_map/ij,jabc->iabc/dot_general | solution.py:150
  171.1 1.3 fusion.132
  172.4 1.9 collective-permute-start.4
  174.3 9.7 %collective-permute-start.5 = (f32[4,1,256,128]{3,0,2,1:T(4,128)S(1)}, f32[4,1,256,128]{3,0,2,1:T(4,128)S(1)}, u32[]{:S(2)}, u32[]{:S(2)}) collective-permute-start(f32[4,1,256,128]{3,0,2,1:T(4,128)S(1)} %get-tuple-element.11), channel_id=1, source_target_pairs={{0,1},{1,2},{2,3},{3,4},{4,5},{5,6},{6,7},{7,8},{8,9},{9,10},{10,1... | collective-permute-start | bytes 1572872 | tf_op jit(solution)/shard_map/ppermute | solution.py:25
  184.1 13.2 %fusion.36 = f32[8,256,128,4]{2,3,1,0:T(4,128)S(1)} fusion(f32[4,4,1,1]{1,0,3,2:T(4,128)S(1)} %copy-done.8, f32[4,8,256,128]{3,0,2,1:T(4,128)} %add_bitcast_fusion, f32[8,256,128,4]{2,3,1,0:T(4,128)} %fusion.43, f32[8,256,128]{2,1,0:T(8,128)} %param.7), kind=kOutput, calls=%fused_computation.64 | convolution fusion | flops 62914560 | bytes 13631552 | tf_op jit(solution)/shard_map/ij,jabc->iabc/dot_general | solution.py:151
  197.3 1.4 fusion.66
  198.7 1.5 copy.14
  200.3 0.8 copy-done.6
  201.1 9.3 %select_maximum_fusion = f32[4,10,258,130]{3,0,2,1:T(4,128)S(1)} fusion(f32[4,1,256,128]{3,0,2,1:T(4,128)S(1)} %collective-permute-done.4, f32[4,8,256,128]{3,0,2,1:T(4,128)S(1)} %copy-done, f32[4,1,256,128]{3,0,2,1:T(4,128)S(1)} %collective-permute-done.5), kind=kLoop, calls=%fused_computation.4 | loop fusion | flops 20124000 | bytes 10609280 | tf_op jit(solution)/shard_map/concatenate | solution.py:29
  210.4 21.1 %fusion.54 = f32[8,256,128,4]{2,3,1,0:T(4,128)} fusion(f32[4,4,1,1]{1,0,3,2:T(4,128)S(1)} %copy-done.8, f32[4,8,256,128]{3,0,2,1:T(4,128)} %add_bitcast_fusion, f32[4,10,258,130]{3,0,2,1:T(4,128)S(1)} %select_maximum_fusion, f32[4,1,256,128]{3,0,2,1:T(4,128)} %copy-done.6, f32[4,1,256,128]{3,0,2,1:T(4,128)S(1)} %collective-permute-done.4, ...), kind=kOutput, calls=%fused_computation.81 | convolution fusion | flops 80740352 | bytes 38799360 | tf_op jit(solution)/shard_map/ij,jabc->iabc/dot_general | solution.py:150
  231.4 3.9 %fusion.67 = f32[2,8,256,128]{3,0,2,1:T(2,128)S(1)} fusion(f32[8,256,128,4]{2,3,1,0:T(4,128)} %fusion.54, s32[]{:T(128)S(6)} %select_n.75, f32[8,256,128]{2,1,0:T(8,128)} %param.6), kind=kLoop, calls=%fused_computation.93 | loop fusion | flops 524288 | bytes 5242884 | tf_op jit(solution)/shard_map/dynamic_slice | solution.py:154
  235.3 1.5 copy.13
  (23 shorter events, 0.2 us)
Async XLA Ops:
  10.6 7.1 %copy-start.4 = (s32[8,256,128]{2,1,0:T(8,128)S(1)}, s32[8,256,128]{2,1,0:T(8,128)}, u32[]{:S(2)}) copy-start(s32[8,256,128]{2,1,0:T(8,128)} %param.8) | copy-start | bytes 3145732
  10.6 98.8 %all-to-all-start = ((f32[2,2,16,256,128]{4,1,3,2,0:T(2,128)}), f32[2,2,16,256,128]{4,1,3,2,0:T(2,128)}, u32[]{:S(2)}, u32[]{:S(2)}) async-start(f32[2,2,16,256,128]{4,1,3,2,0:T(2,128)} %broadcast_in_dim.65), calls=%async_computation | async-start | bytes 16777216 | tf_op jit(solution)/shard_map/all_to_all | solution.py:41
  19.0 13.7 %collective-permute-start = (f32[2,1,256,128]{3,2,1,0:T(8,128)}, f32[2,1,256,128]{3,2,1,0:T(8,128)S(1)}, u32[]{:S(2)}, u32[]{:S(2)}) collective-permute-start(f32[2,1,256,128]{3,2,1,0:T(8,128)} %get-tuple-element.16), channel_id=1, source_target_pairs={{1,0},{2,1},{3,2},{4,3},{5,4},{6,5},{7,6},{8,7},{9,8},{10,9},{11,1... | collective-permute-start | bytes 786440 | tf_op jit(solution)/shard_map/ppermute | solution.py:28
  21.6 12.0 %collective-permute-start.2 = (f32[2,1,256,128]{3,2,1,0:T(8,128)S(1)}, f32[2,1,256,128]{3,2,1,0:T(8,128)S(1)}, u32[]{:S(2)}, u32[]{:S(2)}) collective-permute-start(f32[2,1,256,128]{3,2,1,0:T(8,128)S(1)} %get-tuple-element.15), channel_id=1, source_target_pairs={{0,1},{1,2},{2,3},{3,4},{4,5},{5,6},{6,7},{7,8},{8,9},{9,10},{10,1... | collective-permute-start | bytes 786440 | tf_op jit(solution)/shard_map/ppermute | solution.py:25
  39.4 87.0 %copy-start.8 = (f32[4,4,1,1]{1,0,3,2:T(4,128)S(1)}, f32[4,4,1,1]{1,0,3,2:T(4,128)}, u32[]{:S(2)}) copy-start(f32[4,4,1,1]{1,0,3,2:T(4,128)} %constant.61) | copy-start | bytes 196
  114.9 23.7 %collective-permute-start.1 = (f32[4,1,256,128]{3,0,2,1:T(4,128)S(1)}, f32[4,1,256,128]{3,0,2,1:T(4,128)S(1)}, u32[]{:S(2)}, u32[]{:S(2)}) collective-permute-start(f32[4,1,256,128]{3,0,2,1:T(4,128)S(1)} %get-tuple-element.10), channel_id=1, source_target_pairs={{1,0},{2,1},{3,2},{4,3},{5,4},{6,5},{7,6},{8,7},{9,8},{10,9},{11,1... | collective-permute-start | bytes 1572872 | tf_op jit(solution)/shard_map/ppermute | solution.py:28
  118.3 20.2 %collective-permute-start.3 = (f32[4,1,256,128]{3,0,2,1:T(4,128)S(1)}, f32[4,1,256,128]{3,0,2,1:T(4,128)S(1)}, u32[]{:S(2)}, u32[]{:S(2)}) collective-permute-start(f32[4,1,256,128]{3,0,2,1:T(4,128)S(1)} %get-tuple-element.9), channel_id=1, source_target_pairs={{0,1},{1,2},{2,3},{3,4},{4,5},{5,6},{6,7},{7,8},{8,9},{9,10},{10,1... | collective-permute-start | bytes 1572872 | tf_op jit(solution)/shard_map/ppermute | solution.py:25
  138.6 10.6 %copy-start.1 = (f32[8,256,128]{2,1,0:T(8,128)S(1)}, f32[8,256,128]{2,1,0:T(8,128)}, u32[]{:S(2)}) copy-start(f32[8,256,128]{2,1,0:T(8,128)} %get-tuple-element.13) | copy-start | bytes 3145732
  138.6 10.6 %copy-start.7 = (f32[4,1,256,128]{3,0,2,1:T(4,128)}, f32[4,1,256,128]{3,0,2,1:T(4,128)S(1)}, u32[]{:S(2)}) copy-start(f32[4,1,256,128]{3,0,2,1:T(4,128)S(1)} %collective-permute-done.3) | copy-start | bytes 1572868
  172.4 27.8 %collective-permute-start.4 = (f32[4,1,256,128]{3,0,2,1:T(4,128)S(1)}, f32[4,1,256,128]{3,0,2,1:T(4,128)S(1)}, u32[]{:S(2)}, u32[]{:S(2)}) collective-permute-start(f32[4,1,256,128]{3,0,2,1:T(4,128)S(1)} %get-tuple-element.12), channel_id=1, source_target_pairs={{1,0},{2,1},{3,2},{4,3},{5,4},{6,5},{7,6},{8,7},{9,8},{10,9},{11,1... | collective-permute-start | bytes 1572872 | tf_op jit(solution)/shard_map/ppermute | solution.py:28
  174.3 22.9 %copy-start.5 = (f32[8,256,128]{2,1,0:T(8,128)S(1)}, f32[8,256,128]{2,1,0:T(8,128)}, u32[]{:S(2)}) copy-start(f32[8,256,128]{2,1,0:T(8,128)} %param.7) | copy-start | bytes 3145732
  174.3 25.9 %collective-permute-start.5 = (f32[4,1,256,128]{3,0,2,1:T(4,128)S(1)}, f32[4,1,256,128]{3,0,2,1:T(4,128)S(1)}, u32[]{:S(2)}, u32[]{:S(2)}) collective-permute-start(f32[4,1,256,128]{3,0,2,1:T(4,128)S(1)} %get-tuple-element.11), channel_id=1, source_target_pairs={{0,1},{1,2},{2,3},{3,4},{4,5},{5,6},{6,7},{7,8},{8,9},{9,10},{10,1... | collective-permute-start | bytes 1572872 | tf_op jit(solution)/shard_map/ppermute | solution.py:25
  197.3 3.8 %copy-start = (f32[4,8,256,128]{3,0,2,1:T(4,128)S(1)}, f32[4,8,256,128]{3,0,2,1:T(4,128)}, u32[]{:S(2)}) copy-start(f32[4,8,256,128]{3,0,2,1:T(4,128)} %add_bitcast_fusion) | copy-start | bytes 12582916
  200.2 10.1 %copy-start.2 = (f32[8,256,128]{2,1,0:T(8,128)S(1)}, f32[8,256,128]{2,1,0:T(8,128)}, u32[]{:S(2)}) copy-start(f32[8,256,128]{2,1,0:T(8,128)} %get-tuple-element.14) | copy-start | bytes 3145732
  200.2 10.1 %copy-start.3 = (f32[8,256,128]{2,1,0:T(8,128)S(1)}, f32[8,256,128]{2,1,0:T(8,128)}, u32[]{:S(2)}) copy-start(f32[8,256,128]{2,1,0:T(8,128)} %get-tuple-element.17) | copy-start | bytes 3145732
  200.2 0.8 copy-start.6
where the time goes:
time: 237 us
  waiting for transfers between devices  73.3 us (31%)
  matrix products  68.1 us (29%)
  starting transfers between devices  41.4 us (17%)
  other arithmetic  34.8 us (15%)
  local copies, waits for them, and re-layouts  18.4 us (8%)
    all_to_all x1, waiting for transfers between devices, from_everyone(): lax.all_to_all(jnp.broadcast_to(shard[None], (count, *shard.shape)), axis...  70 us
    dot_general x2, matrix products, on_device(): jnp.einsum('ij,jabc->iabc', weights_all, rate_u, precision=lax.Precision....  43 us
    ppermute x3, starting transfers between devices, with_halo(): lax.ppermute(lax.slice_in_dim(block, block.shape[dim] - width, None, axis...  26.4 us
    dot_general x2, matrix products, on_device(): jnp.einsum('ij,jabc->iabc', weights_all, rate_v, precision=lax.Precision....  25.1 us
    concatenate x2, other arithmetic, with_halo(): block = jnp.concatenate([low, block, high], axis=dim)  19.9 us
    ppermute x3, starting transfers between devices, with_halo(): lax.ppermute(lax.slice_in_dim(block, 0, width, axis=dim), axis, backward)  7.93 us
    all_to_all x1, starting transfers between devices, from_everyone(): lax.all_to_all(jnp.broadcast_to(shard[None], (count, *shard.shape)), axis...  7.07 us
    all_to_all x1, local copies, waits for them, and re-layouts, from_everyone(): lax.all_to_all(jnp.broadcast_to(shard[None], (count, *shard.shape)), axis...  5.38 us
  transfers between devices with their start and end apart: 7, of which 3 were waited for; matrix products, arithmetic and copies ran while one was open for 15% of the time, Pallas kernels for 0%

commit v1 on v0

v1 whole, which is shorter than its diff:
```python
import jax
import jax.numpy as jnp
from jax import lax
from jax.experimental import pallas as pl
from jax.experimental.pallas import tpu as pltpu
from jax.sharding import PartitionSpec as P

MESH = pl.DeviceIdType.MESH
LANES = 128
CHUNK = 16
EDGE = 8
LAG = 2

radau_points = (0.08858795951270396, 0.4094668644407347, 0.7876594617608471, 1.0)
time_step = 0.16
onset_level = 0.15
ionic_gain = 8.0
recovery_base = 0.002
recovery_slope = 0.2
recovery_offset = 0.3
conductances = (1.0, 0.35, 0.05)
excitability = (1.0, 0.6, 0.0)


def weight_table():
    table = []
    for target in range(4):
        entries = []
        for column in range(4):
            coeffs = [1.0]
            for other in range(4):
                if other != column:
                    factor = 1.0 / (radau_points[column] - radau_points[other])
                    raised = [0.0] + coeffs
                    lowered = coeffs + [0.0]
                    coeffs = [
                        factor * (raised[place] - radau_points[other] * lowered[place])
                        for place in range(len(raised))
                    ]
            integral = 0.0
            for place in range(len(coeffs)):
                integral = integral + coeffs[place] * radau_points[target] ** (place + 1) / (
                    place + 1
                )
            entries.append(time_step * integral)
        table.append(entries)
    return table


def label_values(labels, values, outside):
    return jnp.where(
        labels == 0,
        jnp.float32(values[0]),
        jnp.where(
            labels == 1,
            jnp.float32(values[1]),
            jnp.where(labels == 2, jnp.float32(values[2]), jnp.float32(outside)),
        ),
    )


def kernel(
    us_hbm,
    vs_hbm,
    lab_hbm,
    ug_hbm,
    vg_hbm,
    out_u,
    out_v,
    u0,
    u1,
    v,
    res,
    us,
    vs,
    lab,
    cond,
    face,
    exc,
    b0s,
    b0r,
    b1s,
    b1r,
    load_sem,
    lab_send,
    lab_recv,
    own_send,
    own_recv,
    fwd_send,
    fwd_recv,
    mid_send,
    mid_recv,
    row_send,
    row_recv,
    in_send,
    in_recv,
    back_send,
    back_recv,
):
    depth, rows = lab_hbm.shape[0], lab_hbm.shape[1] // 2
    chunks = rows // CHUNK
    node, here = lax.axis_index("node"), lax.axis_index("space")
    count = lax.axis_size("space")
    fold = count // 2
    half = lax.rem(node + here // fold, 2)
    own, other = half * rows, (1 - half) * rows
    has = (here > 0, here < count - 1)
    flips = ((here == fold).astype(jnp.int32), (here == fold - 1).astype(jnp.int32))
    sides = (
        (lax.rem(node + flips[0], 2), here - 1),
        (lax.rem(node + flips[1], 2), here + 1),
    )
    partner = (1 - node, here)
    ours = (1, depth)
    theirs = (depth + 1, 0)

    def mine(k):
        return k * half + (chunks - 1 - k) * (1 - half)

    def its(k):
        return k * (1 - half) + (chunks - 1 - k) * half

    def rows_of(c, base):
        return pl.ds(pl.multiple_of(base + CHUNK * c, 8), CHUNK)

    def remote(src, dst, send, recv, device):
        return pltpu.make_async_remote_copy(
            src_ref=src,
            dst_ref=dst,
            send_sem=send,
            recv_sem=recv,
            device_id=device,
            device_id_type=MESH,
        )

    own_rows = pl.ds(pl.multiple_of(own, 8), rows)
    inner = pl.ds(EDGE, rows)
    slab = pl.ds(1, depth)
    edge_source = pl.ds(pl.multiple_of(rows - EDGE * half, 8), EDGE)
    edge_place = pl.ds(pl.multiple_of((EDGE + rows) * (1 - half), 8), EDGE)
    void_place = pl.ds(pl.multiple_of((EDGE + rows) * half, 8), EDGE)

    def lab_copy(side):
        return remote(
            lab_hbm.at[pl.ds(ours[side] - 1, 1), own_rows],
            lab.at[pl.ds(theirs[side], 1), inner],
            lab_send.at[side],
            lab_recv.at[1 - side],
            sides[side],
        )

    def own_copy(side):
        return remote(
            ug_hbm.at[:, pl.ds(ours[side] - 1, 1), own_rows],
            u0.at[pl.ds(2 * flips[side], 2), pl.ds(theirs[side], 1), inner],
            own_send.at[side],
            own_recv.at[1 - side],
            sides[side],
        )

    def fwd_copy(side, k):
        at = rows_of(mine(k), EDGE)
        return remote(
            u0.at[pl.ds(2, 2), pl.ds(ours[side], 1), at],
            u0.at[pl.ds(2 - 2 * flips[side], 2), pl.ds(theirs[side], 1), at],
            fwd_send.at[side, k],
            fwd_recv.at[1 - side, k],
            sides[side],
        )

    def mid_copy(side, pair, k):
        at = rows_of(mine(k), EDGE)
        to = 2 * (pair + flips[side] - 2 * pair * flips[side])
        return remote(
            u1.at[pl.ds(2 * pair, 2), pl.ds(ours[side], 1), at],
            u1.at[pl.ds(to, 2), pl.ds(theirs[side], 1), at],
            mid_send.at[side, pair, k],
            mid_recv.at[1 - side, pair, k],
            sides[side],
        )

    def in_copy(field, k, c, base):
        return remote(
            (ug_hbm, vg_hbm)[field].at[:, :, rows_of(c, base)],
            (
                u0.at[pl.ds(2, 2), slab, rows_of(c, EDGE)],
                v.at[pl.ds(2, 2), :, rows_of(c, 0)],
            )[field],
            in_send.at[field, k],
            in_recv.at[field, k],
            partner,
        )

    def sent(field, k):
        return in_copy(field, k, its(k), other)

    def arriving(field, k):
        return in_copy(field, k, mine(k), own)

    def back_copies(k, base, c):
        return (
            remote(
                res.at[:, :, rows_of(c, 0)],
                out_u.at[:, :, rows_of(c, base)],
                back_send.at[0, k],
                back_recv.at[0, k],
                partner,
            ),
            remote(
                v.at[pl.ds(2, 2), :, rows_of(c, 0)],
                out_v.at[:, :, rows_of(c, base)],
                back_send.at[1, k],
                back_recv.at[1, k],
                partner,
            ),
        )

    row_copies = (
        remote(b0s, b0r, row_send.at[0], row_recv.at[0], partner),
        remote(b1s, b1r, row_send.at[1], row_recv.at[1], partner),
    )

    loads = [
        pltpu.make_async_copy(src, dst, load_sem.at[i])
        for i, (src, dst) in enumerate(
            (
                (ug_hbm.at[:, :, own_rows], u0.at[pl.ds(0, 2), slab, inner]),
                (lab_hbm.at[:, own_rows], lab.at[slab, inner]),
                (lab_hbm.at[:, edge_source], lab.at[slab, edge_place]),
                (ug_hbm.at[:, :, edge_source], u0.at[pl.ds(0, 2), slab, edge_place]),
                (vg_hbm.at[:, :, own_rows], v.at[pl.ds(0, 2)]),
                (us_hbm.at[:, own_rows], us),
                (vs_hbm.at[:, own_rows], vs),
            )
        )
    ]

    barrier = pltpu.get_barrier_semaphore()
    pl.semaphore_signal(barrier, inc=1, device_id=partner, device_id_type=MESH)
    for side in (0, 1):

        @pl.when(has[side])
        def _():
            pl.semaphore_signal(barrier, inc=1, device_id=sides[side], device_id_type=MESH)

    loads[0].start()
    pl.semaphore_wait(barrier, 1 + has[0].astype(jnp.int32) + has[1].astype(jnp.int32))

    for k in (0, 1):
        sent(0, k).start()
    for copy in loads[1:]:
        copy.start()
    for side in (0, 1):

        @pl.when(has[side])
        def _():
            lab_copy(side).start()
            own_copy(side).start()

    def take_row(source, target, nodes):
        @pl.when(half == 0)
        def _():
            for j in range(nodes):
                for p in range(depth):
                    target[j, p : p + 1] = source[j, p + 1, EDGE + rows - 1 : EDGE + rows]

        @pl.when(half == 1)
        def _():
            for j in range(nodes):
                for p in range(depth):
                    target[j, p : p + 1] = source[j, p + 1, EDGE : EDGE + 1]

    def put_row(source, target, nodes, first):
        @pl.when(half == 0)
        def _():
            for j in range(nodes):
                for p in range(depth):
                    target[first(j), p + 1, EDGE + rows : EDGE + rows + 1] = source[j, p : p + 1]

        @pl.when(half == 1)
        def _():
            for j in range(nodes):
                for p in range(depth):
                    target[first(j), p + 1, EDGE - 1 : EDGE] = source[j, p : p + 1]

    loads[0].wait()
    take_row(u0, b0s, 2)
    row_copies[0].start()

    @pl.loop(2, chunks)
    def _(k):
        sent(0, k).start()

    @pl.loop(0, chunks)
    def _(k):
        sent(1, k).start()

    for place in range(4):
        for p in range(depth):
            u0[place, p + 1, void_place] = jnp.zeros((EDGE, LANES), jnp.float32)
            u1[place, p + 1, void_place] = jnp.zeros((EDGE, LANES), jnp.float32)
    for p in range(depth):
        lab[p + 1, void_place] = jnp.full((EDGE, LANES), 3, jnp.int32)
    for side in (0, 1):

        @pl.when(jnp.logical_not(has[side]))
        def _():
            plane = (0, depth + 1)[side]

            @pl.loop(0, chunks)
            def _(c):
                at = rows_of(c, EDGE)
                lab[plane, at] = jnp.full((CHUNK, LANES), 3, jnp.int32)
                for place in range(4):
                    u0[place, plane, at] = jnp.zeros((CHUNK, LANES), jnp.float32)
                    u1[place, plane, at] = jnp.zeros((CHUNK, LANES), jnp.float32)

    loads[1].wait()
    loads[2].wait()
    for side in (0, 1):

        @pl.when(has[side])
        def _():
            lab_copy(1 - side).wait_recv()

    @pl.loop(0, depth + 2)
    def _(p):
        for c in range(chunks):
            at = pl.ds(EDGE + CHUNK * c, CHUNK)
            cond[p, at] = label_values(lab[p, at], conductances, 0.0)

    for p in range(depth):
        for at in (pl.ds(0, EDGE), pl.ds(EDGE + rows, EDGE)):
            cond[p + 1, at] = label_values(lab[p + 1, at], conductances, 0.0)

    lane = lax.broadcasted_iota(jnp.int32, (CHUNK, LANES), 1)

    @pl.loop(0, depth)
    def _(p):
        @pl.loop(0, chunks)
        def _(c):
            at, to = rows_of(c, EDGE), rows_of(c, 0)
            row = EDGE + CHUNK * c
            center = cond[p + 1, at]
            beside = (
                cond[p + 2, at],
                cond[p, at],
                cond[p + 1, pl.ds(row + 1, CHUNK)],
                cond[p + 1, pl.ds(row - 1, CHUNK)],
                jnp.where(lane == LANES - 1, 0.0, pltpu.roll(center, LANES - 1, 1)),
                jnp.where(lane == 0, 0.0, pltpu.roll(center, 1, 1)),
            )
            total = jnp.zeros_like(center)
            for i in range(6):
                value = 2.0 * center * beside[i] / (center + beside[i])
                face[i, p, to] = value
                total = total + value
            face[6, p, to] = total
            exc[p, to] = label_values(lab[p + 1, at], excitability, 0.0)

    for copy in loads[3:]:
        copy.wait()
    row_copies[0].wait_recv()
    put_row(b0r, u0, 2, lambda j: 2 + j)

    @pl.loop(0, chunks)
    def _(k):
        arriving(0, k).wait_recv()
        for side in (0, 1):

            @pl.when(has[side])
            def _():
                fwd_copy(side, k).start()

    for side in (0, 1):

        @pl.when(has[side])
        def _():
            own_copy(1 - side).wait_recv()

    table = weight_table()
    weights = [
        [
            jnp.where(
                node == 0,
                jnp.float32(table[m][j]),
                jnp.float32(table[(m + 2) % 4][(j + 2) % 4]),
            )
            for j in range(4)
        ]
        for m in range(4)
    ]

    def sweep(source, c, write):
        at, to = rows_of(c, EDGE), rows_of(c, 0)
        row = EDGE + CHUNK * c

        @pl.loop(0, depth)
        def _(p):
            faces = [face[i, p, to] for i in range(7)]
            excite = exc[p, to]
            sum_u = [us[p, to]] * 4
            sum_v = [vs[p, to]] * 4
            for j in range(4):
                mid = source[j, p + 1, at]
                v_mid = v[j, p, to]
                spread = (
                    faces[0] * source[j, p + 2, at]
                    + faces[1] * source[j, p, at]
                    + faces[2] * source[j, p + 1, pl.ds(row + 1, CHUNK)]
                    + faces[3] * source[j, p + 1, pl.ds(row - 1, CHUNK)]
                    + faces[4] * pltpu.roll(mid, LANES - 1, 1)
                    + faces[5] * pltpu.roll(mid, 1, 1)
                )
                scaled = ionic_gain * mid
                growth = (scaled - ionic_gain * onset_level) * (1.0 - mid) - v_mid
                rate_u = spread + mid * (excite * growth - faces[6])
                recovery = recovery_base + recovery_slope * v_mid / jnp.maximum(
                    mid + recovery_offset, recovery_offset
                )
                rate_v = recovery * (-v_mid - scaled * (mid - (onset_level + 1.0)))
                for m in range(4):
                    sum_u[m] = sum_u[m] + weights[m][j] * rate_u
                    sum_v[m] = sum_v[m] + weights[m][j] * rate_v
            write(p, sum_u, sum_v)

    def first_sweep(k):
        c = mine(k)
        at, to = rows_of(c, EDGE), rows_of(c, 0)

        def write(p, new_u, new_v):
            for m in range(4):
                u1[m, p + 1, at] = new_u[m]
                v[m, p, to] = new_v[m]

        sweep(u0, c, write)

    def second_sweep(k):
        c = mine(k)
        to, full = rows_of(c, 0), rows_of(c, own)
        for side in (0, 1):

            @pl.when(has[side])
            def _():
                for pair in (0, 1):
                    mid_copy(1 - side, pair, k).wait_recv()

        def write(p, new_u, new_v):
            for m in range(2):
                out_u[m, p, full] = new_u[m]
                out_v[m, p, full] = new_v[m]
                res[m, p, to] = new_u[2 + m]
                v[2 + m, p, to] = new_v[2 + m]

        sweep(u1, c, write)
        for copy in back_copies(k, own, c):
            copy.start()

    @pl.loop(0, chunks)
    def _(k):
        arriving(1, k).wait_recv()
        for side in (0, 1):

            @pl.when(has[side])
            def _():
                fwd_copy(1 - side, k).wait_recv()

        first_sweep(k)
        for side in (0, 1):

            @pl.when(has[side])
            def _():
                for pair in (0, 1):
                    mid_copy(side, pair, k).start()

        @pl.when(k == 0)
        def _():
            take_row(u1, b1s, 4)
            row_copies[1].start()

        @pl.when(k > LAG)
        def _():
            second_sweep(k - LAG)

    @pl.loop(chunks - LAG, chunks)
    def _(k):
        second_sweep(k)

    row_copies[1].wait_recv()
    put_row(b1r, u1, 4, lambda j: (j + 2) % 4)
    second_sweep(0)

    @pl.loop(0, chunks)
    def _(k):
        for field in (0, 1):
            sent(field, k).wait_send()
        for copy in back_copies(k, own, mine(k)):
            copy.wait_send()
        for side in (0, 1):

            @pl.when(has[side])
            def _():
                fwd_copy(side, k).wait_send()
                for pair in (0, 1):
                    mid_copy(side, pair, k).wait_send()

    for copy in row_copies:
        copy.wait_send()
    for side in (0, 1):

        @pl.when(has[side])
        def _():
            lab_copy(side).wait_send()
            own_copy(side).wait_send()

    @pl.loop(0, chunks)
    def _(k):
        for copy in back_copies(k, other, its(k)):
            copy.wait_recv()


def on_device(*arguments):
    labels = arguments[2]
    depth, width = labels.shape[0], labels.shape[1]
    rows = width // 2
    chunks = rows // CHUNK
    tall = rows + 2 * EDGE
    f32 = jnp.float32
    hbm = pl.BlockSpec(memory_space=pltpu.HBM)
    vmem = pl.BlockSpec(memory_space=pltpu.VMEM)
    dma = pltpu.SemaphoreType.DMA
    result = jax.ShapeDtypeStruct((2, depth, width, LANES), f32)
    return pl.pallas_call(
        kernel,
        out_shape=(result, result),
        in_specs=[hbm] * 5,
        out_specs=(vmem, vmem),
        scratch_shapes=[
            pltpu.VMEM((4, depth + 2, tall, LANES), f32),
            pltpu.VMEM((4, depth + 2, tall, LANES), f32),
            pltpu.VMEM((4, depth, rows, LANES), f32),
            pltpu.VMEM((2, depth, rows, LANES), f32),
            pltpu.VMEM((depth, rows, LANES), f32),
            pltpu.VMEM((depth, rows, LANES), f32),
            pltpu.VMEM((depth + 2, tall, LANES), jnp.int32),
            pltpu.VMEM((depth + 2, tall, LANES), f32),
            pltpu.VMEM((7, depth, rows, LANES), f32),
            pltpu.VMEM((depth, rows, LANES), f32),
            pltpu.VMEM((2, depth, LANES), f32),
            pltpu.VMEM((2, depth, LANES), f32),
            pltpu.VMEM((4, depth, LANES), f32),
            pltpu.VMEM((4, depth, LANES), f32),
            dma((7,)),
            dma((2,)),
            dma((2,)),
            dma((2,)),
            dma((2,)),
            dma((2, chunks)),
            dma((2, chunks)),
            dma((2, 2, chunks)),
            dma((2, 2, chunks)),
            dma((2,)),
            dma((2,)),
            dma((2, chunks)),
            dma((2, chunks)),
            dma((2, chunks)),
            dma((2, chunks)),
        ],
        compiler_params=pltpu.CompilerParams(
            collective_id=0, has_side_effects=True, vmem_limit_bytes=24 * 1024 * 1024
        ),
    )(*[pltpu.with_memory_space_constraint(x, pltpu.HBM) for x in arguments])


def solution(mesh):
    return jax.shard_map(
        on_device,
        mesh=mesh,
        in_specs=(
            P("space", None, None),
            P("space", None, None),
            P("space", None, None),
            P("node", "space", None, None),
            P("node", "space", None, None),
        ),
        out_specs=(P("node", "space", None, None), P("node", "space", None, None)),
        check_vma=False,
    )
```

time: 237 us -> 101 us (0.43)
  the two profiles are of different devices: /device:TPU:231 before, /device:TPU:97 now
where the time goes in v1:
time: 101 us; the launch traced here: 99.2 us
  Pallas kernels  96 us (95%)
  local copies, waits for them, and re-layouts  2.64 us (3%)
    pallas_call x1, Pallas kernels, on_device(): pl.pallas_call(kernel, out_shape=(result, result), in_specs=[hbm] * 5, ou...  96 us
    unnamed x2, local copies, waits for them, and re-layouts  2.64 us

profile of v1, /device:TPU:97, one launch (start us, length us, event | category | flops | bytes accessed | tf_op | source)
XLA Modules:
  0.0 99.2 jit_solution(9207249999964056500)
XLA Ops:
  0.6 96.0 %shard_map.68 = (f32[2,8,256,128]{3,2,1,0:T(8,128)S(1)}, f32[2,8,256,128]{3,2,1,0:T(8,128)S(1)}) custom-call(f32[8,256,128]{2,1,0:T(8,128)} %us_hbm.1, f32[8,256,128]{2,1,0:T(8,128)} %vs_hbm.1, s32[8,256,128]{2,1,0:T(8,128)} %lab_hbm.1, f32[2,8,256,128]{3,2,1,0:T(8,128)} %ug_hbm.1, f32[2,8,256,128]{3,2,1,0:T(8,128)} %vg_hbm.1), custom_call_target="tpu_custom_call" | custom-call | tf_op jit(solution)/shard_map/pallas_call | solution.py:533
  96.6 1.3 %copy.9 = f32[2,8,256,128]{3,2,1,0:T(8,128)} copy(f32[2,8,256,128]{3,2,1,0:T(8,128)S(1)} %get-tuple-element.4) | data formatting | bytes 4194304
  97.9 1.3 %copy.10 = f32[2,8,256,128]{3,2,1,0:T(8,128)} copy(f32[2,8,256,128]{3,2,1,0:T(8,128)S(1)} %get-tuple-element.5) | data formatting | bytes 4194304

commit v2 on v1

--- a/solution.py
+++ b/solution.py
@@ -7,9 +7,10 @@
 
 MESH = pl.DeviceIdType.MESH
 LANES = 128
-CHUNK = 16
+CHUNK = 32
+STEP = 16
 EDGE = 8
-LAG = 2
+LAG = 1
 
 radau_points = (0.08858795951270396, 0.4094668644407347, 0.7876594617608471, 1.0)
 time_step = 0.16
@@ -84,11 +85,8 @@
     load_sem,
     lab_send,
     lab_recv,
-    own_send,
-    own_recv,
-    fwd_send,
-    fwd_recv,
-    mid_send,
+    side_send,
+    halo_recv,
     mid_recv,
     row_send,
     row_recv,
@@ -123,6 +121,9 @@
     def rows_of(c, base):
         return pl.ds(pl.multiple_of(base + CHUNK * c, 8), CHUNK)
 
+    def step_of(row):
+        return pl.ds(pl.multiple_of(row, 8), STEP)
+
     def remote(src, dst, send, recv, device):
         return pltpu.make_async_remote_copy(
             src_ref=src,
@@ -153,8 +154,8 @@
         return remote(
             ug_hbm.at[:, pl.ds(ours[side] - 1, 1), own_rows],
             u0.at[pl.ds(2 * flips[side], 2), pl.ds(theirs[side], 1), inner],
-            own_send.at[side],
-            own_recv.at[1 - side],
+            side_send.at[side],
+            halo_recv.at[1 - side],
             sides[side],
         )
 
@@ -163,8 +164,8 @@
         return remote(
             u0.at[pl.ds(2, 2), pl.ds(ours[side], 1), at],
             u0.at[pl.ds(2 - 2 * flips[side], 2), pl.ds(theirs[side], 1), at],
-            fwd_send.at[side, k],
-            fwd_recv.at[1 - side, k],
+            side_send.at[side],
+            halo_recv.at[1 - side],
             sides[side],
         )
 
@@ -174,8 +175,8 @@
         return remote(
             u1.at[pl.ds(2 * pair, 2), pl.ds(ours[side], 1), at],
             u1.at[pl.ds(to, 2), pl.ds(theirs[side], 1), at],
-            mid_send.at[side, pair, k],
-            mid_recv.at[1 - side, pair, k],
+            side_send.at[side],
+            mid_recv.at[1 - side, k],
             sides[side],
         )
 
@@ -186,7 +187,7 @@
                 u0.at[pl.ds(2, 2), slab, rows_of(c, EDGE)],
                 v.at[pl.ds(2, 2), :, rows_of(c, 0)],
             )[field],
-            in_send.at[field, k],
+            in_send.at[0],
             in_recv.at[field, k],
             partner,
         )
@@ -197,20 +198,20 @@
     def arriving(field, k):
         return in_copy(field, k, mine(k), own)
 
-    def back_copies(k, base, c):
+    def back_copies(c, base):
         return (
             remote(
                 res.at[:, :, rows_of(c, 0)],
                 out_u.at[:, :, rows_of(c, base)],
-                back_send.at[0, k],
-                back_recv.at[0, k],
+                back_send.at[0],
+                back_recv.at[0],
                 partner,
             ),
             remote(
                 v.at[pl.ds(2, 2), :, rows_of(c, 0)],
                 out_v.at[:, :, rows_of(c, base)],
-                back_send.at[1, k],
-                back_recv.at[1, k],
+                back_send.at[0],
+                back_recv.at[0],
                 partner,
             ),
         )
@@ -222,18 +223,20 @@
 
     loads = [
         pltpu.make_async_copy(src, dst, load_sem.at[i])
-        for i, (src, dst) in enumerate(
-            (
-                (ug_hbm.at[:, :, own_rows], u0.at[pl.ds(0, 2), slab, inner]),
-                (lab_hbm.at[:, own_rows], lab.at[slab, inner]),
-                (lab_hbm.at[:, edge_source], lab.at[slab, edge_place]),
-                (ug_hbm.at[:, :, edge_source], u0.at[pl.ds(0, 2), slab, edge_place]),
-                (vg_hbm.at[:, :, own_rows], v.at[pl.ds(0, 2)]),
-                (us_hbm.at[:, own_rows], us),
-                (vs_hbm.at[:, own_rows], vs),
-            )
+        for i, src, dst in (
+            (0, ug_hbm.at[:, :, own_rows], u0.at[pl.ds(0, 2), slab, inner]),
+            (0, ug_hbm.at[:, :, edge_source], u0.at[pl.ds(0, 2), slab, edge_place]),
+            (1, lab_hbm.at[:, own_rows], lab.at[slab, inner]),
+            (1, lab_hbm.at[:, edge_source], lab.at[slab, edge_place]),
+            (2, vg_hbm.at[:, :, own_rows], v.at[pl.ds(0, 2)]),
+            (2, us_hbm.at[:, own_rows], us),
+            (2, vs_hbm.at[:, own_rows], vs),
         )
     ]
+    grown = pl.ds(pl.multiple_of(EDGE * (1 - half), 8), EDGE + rows)
+
+    def await_bytes(ref, sem):
+        pltpu.make_async_copy(ref, ref, sem).wait()
 
     barrier = pltpu.get_barrier_semaphore()
     pl.semaphore_signal(barrier, inc=1, device_id=partner, device_id_type=MESH)
@@ -243,12 +246,13 @@
         def _():
             pl.semaphore_signal(barrier, inc=1, device_id=sides[side], device_id_type=MESH)
 
-    loads[0].start()
+    for copy in loads[:2]:
+        copy.start()
     pl.semaphore_wait(barrier, 1 + has[0].astype(jnp.int32) + has[1].astype(jnp.int32))
 
-    for k in (0, 1):
+    for k in range(2):
         sent(0, k).start()
-    for copy in loads[1:]:
+    for copy in loads[2:]:
         copy.start()
     for side in (0, 1):
 
@@ -283,7 +287,7 @@
                 for p in range(depth):
                     target[first(j), p + 1, EDGE - 1 : EDGE] = source[j, p : p + 1]
 
-    loads[0].wait()
+    await_bytes(u0.at[pl.ds(0, 2), slab, grown], load_sem.at[0])
     take_row(u0, b0s, 2)
     row_copies[0].start()
 
@@ -315,8 +319,7 @@
                     u0[place, plane, at] = jnp.zeros((CHUNK, LANES), jnp.float32)
                     u1[place, plane, at] = jnp.zeros((CHUNK, LANES), jnp.float32)
 
-    loads[1].wait()
-    loads[2].wait()
+    await_bytes(lab.at[slab, grown], load_sem.at[1])
     for side in (0, 1):
 
         @pl.when(has[side])
@@ -333,33 +336,32 @@
         for at in (pl.ds(0, EDGE), pl.ds(EDGE + rows, EDGE)):
             cond[p + 1, at] = label_values(lab[p + 1, at], conductances, 0.0)
 
-    lane = lax.broadcasted_iota(jnp.int32, (CHUNK, LANES), 1)
+    lane = lax.broadcasted_iota(jnp.int32, (STEP, LANES), 1)
 
     @pl.loop(0, depth)
     def _(p):
-        @pl.loop(0, chunks)
-        def _(c):
-            at, to = rows_of(c, EDGE), rows_of(c, 0)
-            row = EDGE + CHUNK * c
+        @pl.loop(0, rows // STEP)
+        def _(i):
+            at, to = step_of(EDGE + STEP * i), step_of(STEP * i)
+            row = EDGE + STEP * i
             center = cond[p + 1, at]
             beside = (
                 cond[p + 2, at],
                 cond[p, at],
-                cond[p + 1, pl.ds(row + 1, CHUNK)],
-                cond[p + 1, pl.ds(row - 1, CHUNK)],
+                cond[p + 1, pl.ds(row + 1, STEP)],
+                cond[p + 1, pl.ds(row - 1, STEP)],
                 jnp.where(lane == LANES - 1, 0.0, pltpu.roll(center, LANES - 1, 1)),
                 jnp.where(lane == 0, 0.0, pltpu.roll(center, 1, 1)),
             )
             total = jnp.zeros_like(center)
-            for i in range(6):
-                value = 2.0 * center * beside[i] / (center + beside[i])
-                face[i, p, to] = value
+            for f in range(6):
+                value = 2.0 * center * beside[f] / (center + beside[f])
+                face[f, p, to] = value
                 total = total + value
             face[6, p, to] = total
             exc[p, to] = label_values(lab[p + 1, at], excitability, 0.0)
 
-    for copy in loads[3:]:
-        copy.wait()
+    await_bytes(v, load_sem.at[2])
     row_copies[0].wait_recv()
     put_row(b0r, u0, 2, lambda j: 2 + j)
 
@@ -376,7 +378,7 @@
 
         @pl.when(has[side])
         def _():
-            own_copy(1 - side).wait_recv()
+            await_bytes(u0.at[:, pl.ds(theirs[1 - side], 1), inner], halo_recv.at[side])
 
     table = weight_table()
     weights = [
@@ -392,12 +394,12 @@
     ]
 
     def sweep(source, c, write):
-        at, to = rows_of(c, EDGE), rows_of(c, 0)
-        row = EDGE + CHUNK * c
-
-        @pl.loop(0, depth)
-        def _(p):
-            faces = [face[i, p, to] for i in range(7)]
+        @pl.loop(0, depth * (CHUNK // STEP))
+        def _(i):
+            p, first = i % depth, CHUNK * c + STEP * (i // depth)
+            at, to = step_of(EDGE + first), step_of(first)
+            row = EDGE + first
+            faces = [face[f, p, to] for f in range(7)]
             excite = exc[p, to]
             sum_u = [us[p, to]] * 4
             sum_v = [vs[p, to]] * 4
@@ -407,8 +409,8 @@
                 spread = (
                     faces[0] * source[j, p + 2, at]
                     + faces[1] * source[j, p, at]
-                    + faces[2] * source[j, p + 1, pl.ds(row + 1, CHUNK)]
-                    + faces[3] * source[j, p + 1, pl.ds(row - 1, CHUNK)]
+                    + faces[2] * source[j, p + 1, pl.ds(row + 1, STEP)]
+                    + faces[3] * source[j, p + 1, pl.ds(row - 1, STEP)]
                     + faces[4] * pltpu.roll(mid, LANES - 1, 1)
                     + faces[5] * pltpu.roll(mid, 1, 1)
                 )
@@ -422,13 +424,13 @@
                 for m in range(4):
                     sum_u[m] = sum_u[m] + weights[m][j] * rate_u
                     sum_v[m] = sum_v[m] + weights[m][j] * rate_v
-            write(p, sum_u, sum_v)
+            write(p, first, sum_u, sum_v)
 
     def first_sweep(k):
         c = mine(k)
-        at, to = rows_of(c, EDGE), rows_of(c, 0)
-
-        def write(p, new_u, new_v):
+
+        def write(p, first, new_u, new_v):
+            at, to = step_of(EDGE + first), step_of(first)
             for m in range(4):
                 u1[m, p + 1, at] = new_u[m]
                 v[m, p, to] = new_v[m]
@@ -437,15 +439,15 @@
 
     def second_sweep(k):
         c = mine(k)
-        to, full = rows_of(c, 0), rows_of(c, own)
         for side in (0, 1):
 
             @pl.when(has[side])
             def _():
-                for pair in (0, 1):
-                    mid_copy(1 - side, pair, k).wait_recv()
-
-        def write(p, new_u, new_v):
+                at = rows_of(c, EDGE)
+                await_bytes(u1.at[:, pl.ds(theirs[1 - side], 1), at], mid_recv.at[side, k])
+
+        def write(p, first, new_u, new_v):
+            to, full = step_of(first), step_of(own + first)
             for m in range(2):
                 out_u[m, p, full] = new_u[m]
                 out_v[m, p, full] = new_v[m]
@@ -453,18 +455,12 @@
                 v[2 + m, p, to] = new_v[2 + m]
 
         sweep(u1, c, write)
-        for copy in back_copies(k, own, c):
+        for copy in back_copies(c, own):
             copy.start()
 
     @pl.loop(0, chunks)
     def _(k):
         arriving(1, k).wait_recv()
-        for side in (0, 1):
-
-            @pl.when(has[side])
-            def _():
-                fwd_copy(1 - side, k).wait_recv()
-
         first_sweep(k)
         for side in (0, 1):
 
@@ -490,33 +486,18 @@
     put_row(b1r, u1, 4, lambda j: (j + 2) % 4)
     second_sweep(0)
 
-    @pl.loop(0, chunks)
-    def _(k):
-        for field in (0, 1):
-            sent(field, k).wait_send()
-        for copy in back_copies(k, own, mine(k)):
-            copy.wait_send()
-        for side in (0, 1):
-
-            @pl.when(has[side])
-            def _():
-                fwd_copy(side, k).wait_send()
-                for pair in (0, 1):
-                    mid_copy(side, pair, k).wait_send()
+    for side in (0, 1):
+
+        @pl.when(has[side])
+        def _():
+            lab_copy(side).wait_send()
+            await_bytes(u1.at[:, pl.ds(0, 2), inner], side_send.at[side])
 
     for copy in row_copies:
         copy.wait_send()
-    for side in (0, 1):
-
-        @pl.when(has[side])
-        def _():
-            lab_copy(side).wait_send()
-            own_copy(side).wait_send()
-
-    @pl.loop(0, chunks)
-    def _(k):
-        for copy in back_copies(k, other, its(k)):
-            copy.wait_recv()
+    await_bytes(v, in_send.at[0])
+    await_bytes(v, back_send.at[0])
+    await_bytes(v, back_recv.at[0])
 
 
 def on_device(*arguments):
@@ -550,21 +531,18 @@
             pltpu.VMEM((2, depth, LANES), f32),
             pltpu.VMEM((4, depth, LANES), f32),
             pltpu.VMEM((4, depth, LANES), f32),
-            dma((7,)),
+            dma((3,)),
             dma((2,)),
             dma((2,)),
             dma((2,)),
             dma((2,)),
             dma((2, chunks)),
-            dma((2, chunks)),
-            dma((2, 2, chunks)),
-            dma((2, 2, chunks)),
             dma((2,)),
             dma((2,)),
+            dma((1,)),
             dma((2, chunks)),
-            dma((2, chunks)),
-            dma((2, chunks)),
-            dma((2, chunks)),
+            dma((1,)),
+            dma((1,)),
         ],
         compiler_params=pltpu.CompilerParams(
             collective_id=0, has_side_effects=True, vmem_limit_bytes=24 * 1024 * 1024

time: 101 us -> 99.2 us (0.982)
  Pallas kernels: 96 us -> 94.6 us
    pallas_call x1, Pallas kernels: 96 us -> 94.6 us  [on_device(): pl.pallas_call(kernel, out_shape=(result, result), in_specs=[hbm] * 5, ou...]
where the time goes in v2:
time: 99.2 us; the launch traced here: 97.9 us
  Pallas kernels  94.6 us (95%)
  local copies, waits for them, and re-layouts  2.64 us (3%)
    pallas_call x1, Pallas kernels, on_device(): pl.pallas_call(kernel, out_shape=(result, result), in_specs=[hbm] * 5, ou...  94.6 us
    unnamed x2, local copies, waits for them, and re-layouts  2.64 us

profile of v2, /device:TPU:97, one launch (start us, length us, event | category | flops | bytes accessed | tf_op | source)
XLA Modules:
  0.0 97.9 jit_solution(11536628803832808075)
XLA Ops:
  0.6 94.6 %shard_map.68 = (f32[2,8,256,128]{3,2,1,0:T(8,128)S(1)}, f32[2,8,256,128]{3,2,1,0:T(8,128)S(1)}) custom-call(f32[8,256,128]{2,1,0:T(8,128)} %us_hbm.1, f32[8,256,128]{2,1,0:T(8,128)} %vs_hbm.1, s32[8,256,128]{2,1,0:T(8,128)} %lab_hbm.1, f32[2,8,256,128]{3,2,1,0:T(8,128)} %ug_hbm.1, f32[2,8,256,128]{3,2,1,0:T(8,128)} %vg_hbm.1), custom_call_target="tpu_custom_call" | custom-call | tf_op jit(solution)/shard_map/pallas_call | solution.py:514
  95.3 1.3 %copy.9 = f32[2,8,256,128]{3,2,1,0:T(8,128)} copy(f32[2,8,256,128]{3,2,1,0:T(8,128)S(1)} %get-tuple-element.4) | data formatting | bytes 4194304
  96.6 1.3 %copy.10 = f32[2,8,256,128]{3,2,1,0:T(8,128)} copy(f32[2,8,256,128]{3,2,1,0:T(8,128)S(1)} %get-tuple-element.5) | data formatting | bytes 4194304

commit v3 on v2

--- a/solution.py
+++ b/solution.py
@@ -94,6 +94,8 @@
     in_recv,
     back_send,
     back_recv,
+    hello,
+    met,
 ):
     depth, rows = lab_hbm.shape[0], lab_hbm.shape[1] // 2
     chunks = rows // CHUNK
@@ -238,17 +240,32 @@
     def await_bytes(ref, sem):
         pltpu.make_async_copy(ref, ref, sem).wait()
 
+    odd, first = here % 2 == 1, node == 1
+    host = jnp.logical_and(odd, jnp.logical_not(first))
+    guest = jnp.logical_and(odd, first)
     barrier = pltpu.get_barrier_semaphore()
-    pl.semaphore_signal(barrier, inc=1, device_id=partner, device_id_type=MESH)
-    for side in (0, 1):
-
-        @pl.when(has[side])
-        def _():
-            pl.semaphore_signal(barrier, inc=1, device_id=sides[side], device_id_type=MESH)
+
+    def signal(sem, device):
+        pl.semaphore_signal(sem, inc=1, device_id=device, device_id_type=MESH)
 
     for copy in loads[:2]:
         copy.start()
-    pl.semaphore_wait(barrier, 1 + has[0].astype(jnp.int32) + has[1].astype(jnp.int32))
+
+    @pl.when(jnp.logical_not(guest))
+    def _():
+        signal(barrier, partner)
+
+    @pl.when(jnp.logical_not(host))
+    def _():
+        pl.semaphore_wait(barrier, 1)
+
+    @pl.when(guest)
+    def _():
+        signal(hello, partner)
+
+    @pl.when(host)
+    def _():
+        pl.semaphore_wait(hello, 1)
 
     for k in range(2):
         sent(0, k).start()
@@ -256,10 +273,9 @@
         copy.start()
     for side in (0, 1):
 
-        @pl.when(has[side])
-        def _():
-            lab_copy(side).start()
-            own_copy(side).start()
+        @pl.when(jnp.logical_and(has[side], jnp.logical_not(jnp.logical_or(odd, sides[side][0] == 1))))
+        def _():
+            signal(barrier, sides[side])
 
     def take_row(source, target, nodes):
         @pl.when(half == 0)
@@ -298,6 +314,34 @@
     @pl.loop(0, chunks)
     def _(k):
         sent(1, k).start()
+
+    beside_count = has[0].astype(jnp.int32) + has[1].astype(jnp.int32)
+
+    @pl.when(host)
+    def _():
+        pl.semaphore_wait(barrier, beside_count)
+        signal(met, partner)
+
+    @pl.when(guest)
+    def _():
+        pl.semaphore_wait(met, 1)
+
+    for side in (0, 1):
+
+        @pl.when(jnp.logical_and(odd, has[side]))
+        def _():
+            signal(met, sides[side])
+
+    @pl.when(jnp.logical_not(odd))
+    def _():
+        pl.semaphore_wait(met, beside_count)
+
+    for side in (0, 1):
+
+        @pl.when(has[side])
+        def _():
+            lab_copy(side).start()
+            own_copy(side).start()
 
     for place in range(4):
         for p in range(depth):
@@ -500,6 +544,19 @@
     await_bytes(v, back_recv.at[0])
 
 
+def store(u_vmem, v_vmem, u_hbm, v_hbm, sem):
+    copies = [
+        pltpu.make_async_copy(src.at[m, p], dst.at[m, p], sem.at[2 * i + m])
+        for i, (src, dst) in enumerate(((u_vmem, u_hbm), (v_vmem, v_hbm)))
+        for m in range(2)
+        for p in range(u_vmem.shape[1])
+    ]
+    for copy in copies:
+        copy.start()
+    for copy in copies:
+        copy.wait()
+
+
 def on_device(*arguments):
     labels = arguments[2]
     depth, width = labels.shape[0], labels.shape[1]
@@ -511,7 +568,7 @@
     vmem = pl.BlockSpec(memory_space=pltpu.VMEM)
     dma = pltpu.SemaphoreType.DMA
     result = jax.ShapeDtypeStruct((2, depth, width, LANES), f32)
-    return pl.pallas_call(
+    results = pl.pallas_call(
         kernel,
         out_shape=(result, result),
         in_specs=[hbm] * 5,
@@ -543,11 +600,21 @@
             dma((2, chunks)),
             dma((1,)),
             dma((1,)),
+            pltpu.SemaphoreType.REGULAR,
+            pltpu.SemaphoreType.REGULAR,
         ],
         compiler_params=pltpu.CompilerParams(
             collective_id=0, has_side_effects=True, vmem_limit_bytes=24 * 1024 * 1024
         ),
     )(*[pltpu.with_memory_space_constraint(x, pltpu.HBM) for x in arguments])
+    return pl.pallas_call(
+        store,
+        out_shape=(result, result),
+        in_specs=[vmem] * 2,
+        out_specs=(hbm, hbm),
+        scratch_shapes=[dma((4,))],
+        compiler_params=pltpu.CompilerParams(vmem_limit_bytes=1024 * 1024),
+    )(*results)
 
 
 def solution(mesh):

time: 99.2 us -> 96.8 us (0.976)
  local copies, waits for them, and re-layouts: 2.64 us -> 0 us
    unnamed x2 -> x0, local copies, waits for them, and re-layouts: 2.64 us -> none
    pallas_call x0 -> x1, Pallas kernels: none -> 2.02 us  [on_device(): pl.pallas_call(store, out_shape=(result, result), in_specs=[vmem] * 2, ou...]
    pallas_call x1, Pallas kernels: 94.6 us -> 92.9 us  [on_device(): pl.pallas_call(kernel, out_shape=(result, result), in_specs=[hbm] * 5, ou...]
where the time goes in v3:
time: 96.8 us; the launch traced here: 95.6 us
  Pallas kernels  95 us (98%)
    pallas_call x1, Pallas kernels, on_device(): pl.pallas_call(kernel, out_shape=(result, result), in_specs=[hbm] * 5, ou...  92.9 us
    pallas_call x1, Pallas kernels, on_device(): pl.pallas_call(store, out_shape=(result, result), in_specs=[vmem] * 2, ou...  2.02 us

profile of v3, /device:TPU:97, one launch (start us, length us, event | category | flops | bytes accessed | tf_op | source)
XLA Modules:
  0.0 95.6 jit_solution(7484566082959814865)
XLA Ops:
  0.6 92.9 %shard_map.68 = (f32[2,8,256,128]{3,2,1,0:T(8,128)S(1)}, f32[2,8,256,128]{3,2,1,0:T(8,128)S(1)}) custom-call(f32[8,256,128]{2,1,0:T(8,128)} %us_hbm.1, f32[8,256,128]{2,1,0:T(8,128)} %vs_hbm.1, s32[8,256,128]{2,1,0:T(8,128)} %lab_hbm.1, f32[2,8,256,128]{3,2,1,0:T(8,128)} %ug_hbm.1, f32[2,8,256,128]{3,2,1,0:T(8,128)} %vg_hbm.1), custom_call_target="tpu_custom_call" | custom-call | tf_op jit(solution)/shard_map/pallas_call | solution.py:571
  93.6 2.0 %shard_map.69 = (f32[2,8,256,128]{3,2,1,0:T(8,128)}, f32[2,8,256,128]{3,2,1,0:T(8,128)}) custom-call(f32[2,8,256,128]{3,2,1,0:T(8,128)S(1)} %get-tuple-element.4.u_vmem, f32[2,8,256,128]{3,2,1,0:T(8,128)S(1)} %get-tuple-element.5.v_vmem), custom_call_target="tpu_custom_call" | custom-call | tf_op jit(solution)/shard_map/pallas_call | solution.py:610

commit v4 on v3

--- a/solution.py
+++ b/solution.py
@@ -10,7 +10,6 @@
 CHUNK = 32
 STEP = 16
 EDGE = 8
-LAG = 1
 
 radau_points = (0.08858795951270396, 0.4094668644407347, 0.7876594617608471, 1.0)
 time_step = 0.16
@@ -200,18 +199,19 @@
     def arriving(field, k):
         return in_copy(field, k, mine(k), own)
 
-    def back_copies(c, base):
+    def back_copies(row):
+        to, full = step_of(row), step_of(own + row)
         return (
             remote(
-                res.at[:, :, rows_of(c, 0)],
-                out_u.at[:, :, rows_of(c, base)],
+                res.at[:, :, to],
+                out_u.at[:, :, full],
                 back_send.at[0],
                 back_recv.at[0],
                 partner,
             ),
             remote(
-                v.at[pl.ds(2, 2), :, rows_of(c, 0)],
-                out_v.at[:, :, rows_of(c, base)],
+                v.at[pl.ds(2, 2), :, to],
+                out_v.at[:, :, full],
                 back_send.at[0],
                 back_recv.at[0],
                 partner,
@@ -240,7 +240,7 @@
     def await_bytes(ref, sem):
         pltpu.make_async_copy(ref, ref, sem).wait()
 
-    odd, first = here % 2 == 1, node == 1
+    odd, first = here % 2 == 0, node == 1
     host = jnp.logical_and(odd, jnp.logical_not(first))
     guest = jnp.logical_and(odd, first)
     barrier = pltpu.get_barrier_semaphore()
@@ -278,30 +278,20 @@
             signal(barrier, sides[side])
 
     def take_row(source, target, nodes):
-        @pl.when(half == 0)
-        def _():
+        line = EDGE + (rows - 1) * (1 - half)
+
+        @pl.loop(0, depth)
+        def _(p):
             for j in range(nodes):
-                for p in range(depth):
-                    target[j, p : p + 1] = source[j, p + 1, EDGE + rows - 1 : EDGE + rows]
-
-        @pl.when(half == 1)
-        def _():
+                target[j, pl.ds(p, 1)] = source[j, p + 1, pl.ds(line, 1)]
+
+    def put_row(source, target, nodes, first):
+        line = EDGE - 1 + (rows + 1) * (1 - half)
+
+        @pl.loop(0, depth)
+        def _(p):
             for j in range(nodes):
-                for p in range(depth):
-                    target[j, p : p + 1] = source[j, p + 1, EDGE : EDGE + 1]
-
-    def put_row(source, target, nodes, first):
-        @pl.when(half == 0)
-        def _():
-            for j in range(nodes):
-                for p in range(depth):
-                    target[first(j), p + 1, EDGE + rows : EDGE + rows + 1] = source[j, p : p + 1]
-
-        @pl.when(half == 1)
-        def _():
-            for j in range(nodes):
-                for p in range(depth):
-                    target[first(j), p + 1, EDGE - 1 : EDGE] = source[j, p : p + 1]
+                target[first(j), p + 1, pl.ds(line, 1)] = source[j, pl.ds(p, 1)]
 
     await_bytes(u0.at[pl.ds(0, 2), slab, grown], load_sem.at[0])
     take_row(u0, b0s, 2)
@@ -343,12 +333,13 @@
             lab_copy(side).start()
             own_copy(side).start()
 
-    for place in range(4):
-        for p in range(depth):
+    @pl.loop(0, depth)
+    def _(p):
+        lab[p + 1, void_place] = jnp.full((EDGE, LANES), 3, jnp.int32)
+        for place in range(4):
             u0[place, p + 1, void_place] = jnp.zeros((EDGE, LANES), jnp.float32)
             u1[place, p + 1, void_place] = jnp.zeros((EDGE, LANES), jnp.float32)
-    for p in range(depth):
-        lab[p + 1, void_place] = jnp.full((EDGE, LANES), 3, jnp.int32)
+
     for side in (0, 1):
 
         @pl.when(jnp.logical_not(has[side]))
@@ -372,13 +363,15 @@
 
     @pl.loop(0, depth + 2)
     def _(p):
-        for c in range(chunks):
-            at = pl.ds(EDGE + CHUNK * c, CHUNK)
+        @pl.loop(0, chunks)
+        def _(c):
+            at = rows_of(c, EDGE)
             cond[p, at] = label_values(lab[p, at], conductances, 0.0)
 
-    for p in range(depth):
+    @pl.loop(1, depth + 1)
+    def _(p):
         for at in (pl.ds(0, EDGE), pl.ds(EDGE + rows, EDGE)):
-            cond[p + 1, at] = label_values(lab[p + 1, at], conductances, 0.0)
+            cond[p, at] = label_values(lab[p, at], conductances, 0.0)
 
     lane = lax.broadcasted_iota(jnp.int32, (STEP, LANES), 1)
 
@@ -437,10 +430,10 @@
         for m in range(4)
     ]
 
-    def sweep(source, c, write):
-        @pl.loop(0, depth * (CHUNK // STEP))
+    def sweep(source, start, steps, write):
+        @pl.loop(0, depth * steps)
         def _(i):
-            p, first = i % depth, CHUNK * c + STEP * (i // depth)
+            p, first = i % depth, start + STEP * (i // depth)
             at, to = step_of(EDGE + first), step_of(first)
             row = EDGE + first
             faces = [face[f, p, to] for f in range(7)]
@@ -471,25 +464,15 @@
             write(p, first, sum_u, sum_v)
 
     def first_sweep(k):
-        c = mine(k)
-
         def write(p, first, new_u, new_v):
             at, to = step_of(EDGE + first), step_of(first)
             for m in range(4):
                 u1[m, p + 1, at] = new_u[m]
                 v[m, p, to] = new_v[m]
 
-        sweep(u0, c, write)
-
-    def second_sweep(k):
-        c = mine(k)
-        for side in (0, 1):
-
-            @pl.when(has[side])
-            def _():
-                at = rows_of(c, EDGE)
-                await_bytes(u1.at[:, pl.ds(theirs[1 - side], 1), at], mid_recv.at[side, k])
-
+        sweep(u0, CHUNK * mine(k), CHUNK // STEP, write)
+
+    def second_sweep(row):
         def write(p, first, new_u, new_v):
             to, full = step_of(first), step_of(own + first)
             for m in range(2):
@@ -498,37 +481,58 @@
                 res[m, p, to] = new_u[2 + m]
                 v[2 + m, p, to] = new_v[2 + m]
 
-        sweep(u1, c, write)
-        for copy in back_copies(c, own):
+        sweep(u1, row, 1, write)
+        for copy in back_copies(row):
             copy.start()
 
-    @pl.loop(0, chunks)
-    def _(k):
-        arriving(1, k).wait_recv()
-        first_sweep(k)
+    def await_mid(k):
+        at = rows_of(mine(k), EDGE)
         for side in (0, 1):
 
             @pl.when(has[side])
             def _():
-                for pair in (0, 1):
-                    mid_copy(side, pair, k).start()
+                await_bytes(u1.at[:, pl.ds(theirs[1 - side], 1), at], mid_recv.at[side, k])
+
+    each = CHUNK // STEP
+    steps = chunks * each
+
+    @pl.loop(0, chunks + 1)
+    def _(k):
+        @pl.when(k < chunks)
+        def _():
+            arriving(1, k).wait_recv()
+            first_sweep(k)
+            for side in (0, 1):
+
+                @pl.when(has[side])
+                def _():
+                    for pair in (0, 1):
+                        mid_copy(side, pair, k).start()
 
         @pl.when(k == 0)
         def _():
             take_row(u1, b1s, 4)
             row_copies[1].start()
 
-        @pl.when(k > LAG)
-        def _():
-            second_sweep(k - LAG)
-
-    @pl.loop(chunks - LAG, chunks)
-    def _(k):
-        second_sweep(k)
-
-    row_copies[1].wait_recv()
-    put_row(b1r, u1, 4, lambda j: (j + 2) % 4)
-    second_sweep(0)
+        @pl.when(k == 1)
+        def _():
+            await_mid(0)
+
+        @pl.when(jnp.logical_and(k > 0, k < chunks))
+        def _():
+            await_mid(k)
+
+        @pl.when(k == chunks)
+        def _():
+            row_copies[1].wait_recv()
+            put_row(b1r, u1, 4, lambda j: (j + 2) % 4)
+
+        @pl.when(k > 0)
+        def _():
+            @pl.loop(0, each)
+            def _(i):
+                t = lax.rem(each * (k - 1) + 1 + i, steps)
+                second_sweep(STEP * (t * half + (steps - 1 - t) * (1 - half)))
 
     for side in (0, 1):
 

time: 96.8 us -> 96.5 us (level); the launches traced: 95.6 us -> 96.4 us
  no operation moved by 1% of the time
where the time goes in v4:
time: 96.5 us; the launch traced here: 96.4 us
  Pallas kernels  95.8 us (99%)
    pallas_call x1, Pallas kernels, on_device(): pl.pallas_call(kernel, out_shape=(result, result), in_specs=[hbm] * 5, ou...  93.8 us
    pallas_call x1, Pallas kernels, on_device(): pl.pallas_call(store, out_shape=(result, result), in_specs=[vmem] * 2, ou...  2.02 us

profile of v4, /device:TPU:97, one launch (start us, length us, event | category | flops | bytes accessed | tf_op | source)
XLA Modules:
  0.0 96.4 jit_solution(11627278786468714565)
XLA Ops:
  0.6 93.8 %shard_map.68 = (f32[2,8,256,128]{3,2,1,0:T(8,128)S(1)}, f32[2,8,256,128]{3,2,1,0:T(8,128)S(1)}) custom-call(f32[8,256,128]{2,1,0:T(8,128)} %us_hbm.1, f32[8,256,128]{2,1,0:T(8,128)} %vs_hbm.1, s32[8,256,128]{2,1,0:T(8,128)} %lab_hbm.1, f32[2,8,256,128]{3,2,1,0:T(8,128)} %ug_hbm.1, f32[2,8,256,128]{3,2,1,0:T(8,128)} %vg_hbm.1), custom_call_target="tpu_custom_call" | custom-call | tf_op jit(solution)/shard_map/pallas_call | solution.py:575
  94.4 2.0 %shard_map.69 = (f32[2,8,256,128]{3,2,1,0:T(8,128)}, f32[2,8,256,128]{3,2,1,0:T(8,128)}) custom-call(f32[2,8,256,128]{3,2,1,0:T(8,128)S(1)} %get-tuple-element.4.u_vmem, f32[2,8,256,128]{3,2,1,0:T(8,128)S(1)} %get-tuple-element.5.v_vmem), custom_call_target="tpu_custom_call" | custom-call | tf_op jit(solution)/shard_map/pallas_call | solution.py:614

commit v5 on v4

--- a/solution.py
+++ b/solution.py
@@ -77,13 +77,10 @@
     cond,
     face,
     exc,
-    b0s,
+    lines,
     b0r,
-    b1s,
     b1r,
     load_sem,
-    lab_send,
-    lab_recv,
     side_send,
     halo_recv,
     mid_recv,
@@ -146,8 +143,8 @@
         return remote(
             lab_hbm.at[pl.ds(ours[side] - 1, 1), own_rows],
             lab.at[pl.ds(theirs[side], 1), inner],
-            lab_send.at[side],
-            lab_recv.at[1 - side],
+            side_send.at[0],
+            halo_recv.at[0],
             sides[side],
         )
 
@@ -155,18 +152,17 @@
         return remote(
             ug_hbm.at[:, pl.ds(ours[side] - 1, 1), own_rows],
             u0.at[pl.ds(2 * flips[side], 2), pl.ds(theirs[side], 1), inner],
-            side_send.at[side],
-            halo_recv.at[1 - side],
+            side_send.at[0],
+            halo_recv.at[0],
             sides[side],
         )
 
-    def fwd_copy(side, k):
-        at = rows_of(mine(k), EDGE)
+    def fwd_copy(side):
         return remote(
-            u0.at[pl.ds(2, 2), pl.ds(ours[side], 1), at],
-            u0.at[pl.ds(2 - 2 * flips[side], 2), pl.ds(theirs[side], 1), at],
-            side_send.at[side],
-            halo_recv.at[1 - side],
+            u0.at[pl.ds(2, 2), pl.ds(ours[side], 1), inner],
+            u0.at[pl.ds(2 - 2 * flips[side], 2), pl.ds(theirs[side], 1), inner],
+            side_send.at[0],
+            halo_recv.at[0],
             sides[side],
         )
 
@@ -176,8 +172,8 @@
         return remote(
             u1.at[pl.ds(2 * pair, 2), pl.ds(ours[side], 1), at],
             u1.at[pl.ds(to, 2), pl.ds(theirs[side], 1), at],
-            side_send.at[side],
-            mid_recv.at[1 - side, k],
+            side_send.at[0],
+            mid_recv.at[k],
             sides[side],
         )
 
@@ -189,7 +185,7 @@
                 v.at[pl.ds(2, 2), :, rows_of(c, 0)],
             )[field],
             in_send.at[0],
-            in_recv.at[field, k],
+            in_recv.at[k if field else chunks],
             partner,
         )
 
@@ -219,8 +215,8 @@
         )
 
     row_copies = (
-        remote(b0s, b0r, row_send.at[0], row_recv.at[0], partner),
-        remote(b1s, b1r, row_send.at[1], row_recv.at[1], partner),
+        remote(lines.at[pl.ds(0, 2)], b0r, row_send.at[0], row_recv.at[0], partner),
+        remote(lines.at[pl.ds(2, 4)], b1r, row_send.at[0], row_recv.at[1], partner),
     )
 
     loads = [
@@ -240,6 +236,17 @@
     def await_bytes(ref, sem):
         pltpu.make_async_copy(ref, ref, sem).wait()
 
+    both = jnp.logical_and(has[0], has[1])
+
+    def await_sides(few, all_of_them, sem):
+        @pl.when(both)
+        def _():
+            await_bytes(all_of_them, sem)
+
+        @pl.when(jnp.logical_not(both))
+        def _():
+            await_bytes(few, sem)
+
     odd, first = here % 2 == 0, node == 1
     host = jnp.logical_and(odd, jnp.logical_not(first))
     guest = jnp.logical_and(odd, first)
@@ -277,13 +284,13 @@
         def _():
             signal(barrier, sides[side])
 
-    def take_row(source, target, nodes):
+    def take_row(source, place, nodes):
         line = EDGE + (rows - 1) * (1 - half)
 
         @pl.loop(0, depth)
         def _(p):
             for j in range(nodes):
-                target[j, pl.ds(p, 1)] = source[j, p + 1, pl.ds(line, 1)]
+                lines[place + j, pl.ds(p, 1)] = source[j, p + 1, pl.ds(line, 1)]
 
     def put_row(source, target, nodes, first):
         line = EDGE - 1 + (rows + 1) * (1 - half)
@@ -294,7 +301,7 @@
                 target[first(j), p + 1, pl.ds(line, 1)] = source[j, pl.ds(p, 1)]
 
     await_bytes(u0.at[pl.ds(0, 2), slab, grown], load_sem.at[0])
-    take_row(u0, b0s, 2)
+    take_row(u0, 0, 2)
     row_copies[0].start()
 
     @pl.loop(2, chunks)
@@ -354,12 +361,22 @@
                     u0[place, plane, at] = jnp.zeros((CHUNK, LANES), jnp.float32)
                     u1[place, plane, at] = jnp.zeros((CHUNK, LANES), jnp.float32)
 
+    await_bytes(v, load_sem.at[2])
+    row_copies[0].wait_recv()
+    put_row(b0r, u0, 2, lambda j: 2 + j)
+
+    await_bytes(u0.at[pl.ds(2, 2), slab, inner], in_recv.at[chunks])
+    for side in (0, 1):
+
+        @pl.when(has[side])
+        def _():
+            fwd_copy(side).start()
+
+    await_sides(
+        u1.at[0, pl.ds(0, 5), inner], u1.at[0, pl.ds(0, 10), inner], halo_recv.at[0]
+    )
+
     await_bytes(lab.at[slab, grown], load_sem.at[1])
-    for side in (0, 1):
-
-        @pl.when(has[side])
-        def _():
-            lab_copy(1 - side).wait_recv()
 
     @pl.loop(0, depth + 2)
     def _(p):
@@ -397,25 +414,6 @@
                 total = total + value
             face[6, p, to] = total
             exc[p, to] = label_values(lab[p + 1, at], excitability, 0.0)
-
-    await_bytes(v, load_sem.at[2])
-    row_copies[0].wait_recv()
-    put_row(b0r, u0, 2, lambda j: 2 + j)
-
-    @pl.loop(0, chunks)
-    def _(k):
-        arriving(0, k).wait_recv()
-        for side in (0, 1):
-
-            @pl.when(has[side])
-            def _():
-                fwd_copy(side, k).start()
-
-    for side in (0, 1):
-
-        @pl.when(has[side])
-        def _():
-            await_bytes(u0.at[:, pl.ds(theirs[1 - side], 1), inner], halo_recv.at[side])
 
     table = weight_table()
     weights = [
@@ -487,11 +485,7 @@
 
     def await_mid(k):
         at = rows_of(mine(k), EDGE)
-        for side in (0, 1):
-
-            @pl.when(has[side])
-            def _():
-                await_bytes(u1.at[:, pl.ds(theirs[1 - side], 1), at], mid_recv.at[side, k])
+        await_sides(u1.at[:, pl.ds(0, 1), at], u1.at[:, pl.ds(0, 2), at], mid_recv.at[k])
 
     each = CHUNK // STEP
     steps = chunks * each
@@ -511,7 +505,7 @@
 
         @pl.when(k == 0)
         def _():
-            take_row(u1, b1s, 4)
+            take_row(u1, 2, 4)
             row_copies[1].start()
 
         @pl.when(k == 1)
@@ -534,31 +528,23 @@
                 t = lax.rem(each * (k - 1) + 1 + i, steps)
                 second_sweep(STEP * (t * half + (steps - 1 - t) * (1 - half)))
 
-    for side in (0, 1):
-
-        @pl.when(has[side])
-        def _():
-            lab_copy(side).wait_send()
-            await_bytes(u1.at[:, pl.ds(0, 2), inner], side_send.at[side])
-
-    for copy in row_copies:
-        copy.wait_send()
+    await_sides(
+        u1.at[0, pl.ds(0, 9), inner], u1.at[pl.ds(0, 2), pl.ds(0, 9), inner], side_send.at[0]
+    )
+    await_bytes(lines, row_send.at[0])
     await_bytes(v, in_send.at[0])
     await_bytes(v, back_send.at[0])
     await_bytes(v, back_recv.at[0])
 
 
 def store(u_vmem, v_vmem, u_hbm, v_hbm, sem):
-    copies = [
-        pltpu.make_async_copy(src.at[m, p], dst.at[m, p], sem.at[2 * i + m])
-        for i, (src, dst) in enumerate(((u_vmem, u_hbm), (v_vmem, v_hbm)))
-        for m in range(2)
-        for p in range(u_vmem.shape[1])
-    ]
-    for copy in copies:
-        copy.start()
-    for copy in copies:
-        copy.wait()
+    pairs = ((u_vmem, u_hbm), (v_vmem, v_hbm))
+    for i, (src, dst) in enumerate(pairs):
+        for m in range(2):
+            for p in range(u_vmem.shape[1]):
+                pltpu.make_async_copy(src.at[m, p], dst.at[m, p], sem.at[i]).start()
+    for i, (src, dst) in enumerate(pairs):
+        pltpu.make_async_copy(src, dst, sem.at[i]).wait()
 
 
 def on_device(*arguments):
@@ -588,20 +574,17 @@
             pltpu.VMEM((depth + 2, tall, LANES), f32),
             pltpu.VMEM((7, depth, rows, LANES), f32),
             pltpu.VMEM((depth, rows, LANES), f32),
-            pltpu.VMEM((2, depth, LANES), f32),
+            pltpu.VMEM((6, depth, LANES), f32),
             pltpu.VMEM((2, depth, LANES), f32),
             pltpu.VMEM((4, depth, LANES), f32),
-            pltpu.VMEM((4, depth, LANES), f32),
             dma((3,)),
-            dma((2,)),
-            dma((2,)),
-            dma((2,)),
-            dma((2,)),
-            dma((2, chunks)),
-            dma((2,)),
+            dma((1,)),
+            dma((1,)),
+            dma((chunks,)),
+            dma((1,)),
             dma((2,)),
             dma((1,)),
-            dma((2, chunks)),
+            dma((chunks + 1,)),
             dma((1,)),
             dma((1,)),
             pltpu.SemaphoreType.REGULAR,
@@ -616,7 +599,7 @@
         out_shape=(result, result),
         in_specs=[vmem] * 2,
         out_specs=(hbm, hbm),
-        scratch_shapes=[dma((4,))],
+        scratch_shapes=[dma((2,))],
         compiler_params=pltpu.CompilerParams(vmem_limit_bytes=1024 * 1024),
     )(*results)
 

time: 96.5 us -> 96.4 us (level)
  no operation moved by 1% of the time
where the time goes in v5:
time: 96.4 us; the launch traced here: 96.3 us
  Pallas kernels  95.6 us (99%)
    pallas_call x1, Pallas kernels, on_device(): pl.pallas_call(kernel, out_shape=(result, result), in_specs=[hbm] * 5, ou...  93.6 us
    pallas_call x1, Pallas kernels, on_device(): pl.pallas_call(store, out_shape=(result, result), in_specs=[vmem] * 2, ou...  2 us

profile of v5, /device:TPU:97, one launch (start us, length us, event | category | flops | bytes accessed | tf_op | source)
XLA Modules:
  0.0 96.3 jit_solution(2132321375981748732)
XLA Ops:
  0.6 93.6 %shard_map.68 = (f32[2,8,256,128]{3,2,1,0:T(8,128)S(1)}, f32[2,8,256,128]{3,2,1,0:T(8,128)S(1)}) custom-call(f32[8,256,128]{2,1,0:T(8,128)} %us_hbm.1, f32[8,256,128]{2,1,0:T(8,128)} %vs_hbm.1, s32[8,256,128]{2,1,0:T(8,128)} %lab_hbm.1, f32[2,8,256,128]{3,2,1,0:T(8,128)} %ug_hbm.1, f32[2,8,256,128]{3,2,1,0:T(8,128)} %vg_hbm.1), custom_call_target="tpu_custom_call" | custom-call | tf_op jit(solution)/shard_map/pallas_call | solution.py:561
  94.3 2.0 %shard_map.69 = (f32[2,8,256,128]{3,2,1,0:T(8,128)}, f32[2,8,256,128]{3,2,1,0:T(8,128)}) custom-call(f32[2,8,256,128]{3,2,1,0:T(8,128)S(1)} %get-tuple-element.4.u_vmem, f32[2,8,256,128]{3,2,1,0:T(8,128)S(1)} %get-tuple-element.5.v_vmem), custom_call_target="tpu_custom_call" | custom-call | tf_op jit(solution)/shard_map/pallas_call | solution.py:597

commit v6 on v5

--- a/solution.py
+++ b/solution.py
@@ -255,9 +255,6 @@
     def signal(sem, device):
         pl.semaphore_signal(sem, inc=1, device_id=device, device_id_type=MESH)
 
-    for copy in loads[:2]:
-        copy.start()
-
     @pl.when(jnp.logical_not(guest))
     def _():
         signal(barrier, partner)
@@ -276,7 +273,7 @@
 
     for k in range(2):
         sent(0, k).start()
-    for copy in loads[2:]:
+    for copy in loads:
         copy.start()
     for side in (0, 1):
 

time: 96.4 us -> 96.4 us (level)
  no operation moved by 1% of the time
where the time goes in v6:
time: 96.4 us; the launch traced here: 96.3 us
  Pallas kernels  95.6 us (99%)
    pallas_call x1, Pallas kernels, on_device(): pl.pallas_call(kernel, out_shape=(result, result), in_specs=[hbm] * 5, ou...  93.6 us
    pallas_call x1, Pallas kernels, on_device(): pl.pallas_call(store, out_shape=(result, result), in_specs=[vmem] * 2, ou...  2 us

profile of v6, /device:TPU:97, one launch (start us, length us, event | category | flops | bytes accessed | tf_op | source)
XLA Modules:
  0.0 96.3 jit_solution(11016479574895154503)
XLA Ops:
  0.6 93.6 %shard_map.68 = (f32[2,8,256,128]{3,2,1,0:T(8,128)S(1)}, f32[2,8,256,128]{3,2,1,0:T(8,128)S(1)}) custom-call(f32[8,256,128]{2,1,0:T(8,128)} %us_hbm.1, f32[8,256,128]{2,1,0:T(8,128)} %vs_hbm.1, s32[8,256,128]{2,1,0:T(8,128)} %lab_hbm.1, f32[2,8,256,128]{3,2,1,0:T(8,128)} %ug_hbm.1, f32[2,8,256,128]{3,2,1,0:T(8,128)} %vg_hbm.1), custom_call_target="tpu_custom_call" | custom-call | tf_op jit(solution)/shard_map/pallas_call | solution.py:558
  94.3 2.0 %shard_map.69 = (f32[2,8,256,128]{3,2,1,0:T(8,128)}, f32[2,8,256,128]{3,2,1,0:T(8,128)}) custom-call(f32[2,8,256,128]{3,2,1,0:T(8,128)S(1)} %get-tuple-element.4.u_vmem, f32[2,8,256,128]{3,2,1,0:T(8,128)S(1)} %get-tuple-element.5.v_vmem), custom_call_target="tpu_custom_call" | custom-call | tf_op jit(solution)/shard_map/pallas_call | solution.py:594

commit v7 on v5

--- a/solution.py
+++ b/solution.py
@@ -274,8 +274,13 @@
     def _():
         pl.semaphore_wait(hello, 1)
 
-    for k in range(2):
-        sent(0, k).start()
+    remote(
+        ug_hbm.at[:, :, pl.ds(pl.multiple_of(other, 8), rows)],
+        u0.at[pl.ds(2, 2), slab, inner],
+        in_send.at[0],
+        in_recv.at[chunks],
+        partner,
+    ).start()
     for copy in loads[2:]:
         copy.start()
     for side in (0, 1):
@@ -303,10 +308,6 @@
     await_bytes(u0.at[pl.ds(0, 2), slab, grown], load_sem.at[0])
     take_row(u0, 0, 2)
     row_copies[0].start()
-
-    @pl.loop(2, chunks)
-    def _(k):
-        sent(0, k).start()
 
     @pl.loop(0, chunks)
     def _(k):

time: 96.4 us -> 96.4 us (level)
  no operation moved by 1% of the time
where the time goes in v7:
time: 96.4 us; the launch traced here: 96.3 us
  Pallas kernels  95.6 us (99%)
    pallas_call x1, Pallas kernels, on_device(): pl.pallas_call(kernel, out_shape=(result, result), in_specs=[hbm] * 5, ou...  93.6 us
    pallas_call x1, Pallas kernels, on_device(): pl.pallas_call(store, out_shape=(result, result), in_specs=[vmem] * 2, ou...  2 us

profile of v7, /device:TPU:97, one launch (start us, length us, event | category | flops | bytes accessed | tf_op | source)
XLA Modules:
  0.0 96.3 jit_solution(3618144144553843774)
XLA Ops:
  0.6 93.6 %shard_map.68 = (f32[2,8,256,128]{3,2,1,0:T(8,128)S(1)}, f32[2,8,256,128]{3,2,1,0:T(8,128)S(1)}) custom-call(f32[8,256,128]{2,1,0:T(8,128)} %us_hbm.1, f32[8,256,128]{2,1,0:T(8,128)} %vs_hbm.1, s32[8,256,128]{2,1,0:T(8,128)} %lab_hbm.1, f32[2,8,256,128]{3,2,1,0:T(8,128)} %ug_hbm.1, f32[2,8,256,128]{3,2,1,0:T(8,128)} %vg_hbm.1), custom_call_target="tpu_custom_call" | custom-call | tf_op jit(solution)/shard_map/pallas_call | solution.py:562
  94.3 2.0 %shard_map.69 = (f32[2,8,256,128]{3,2,1,0:T(8,128)}, f32[2,8,256,128]{3,2,1,0:T(8,128)}) custom-call(f32[2,8,256,128]{3,2,1,0:T(8,128)S(1)} %get-tuple-element.4.u_vmem, f32[2,8,256,128]{3,2,1,0:T(8,128)S(1)} %get-tuple-element.5.v_vmem), custom_call_target="tpu_custom_call" | custom-call | tf_op jit(solution)/shard_map/pallas_call | solution.py:598
